TPU v7x, 256 devices: a whole 4x4x8 slice. The times are simulated.
256 devices in a mesh: dp: 16 (over y, x), expert: 16 (over z, core).
Axes of the slice: x: 4, y: 4, z: 8, core: 2. Of those that a mesh axis runs over, the one named last changes fastest.
Arguments:
- tokens: bfloat16 [4096, 4096], P('dp', 'expert'), may hold values from -6 to 6
- routing: int32 [4096, 2], P('dp'), may hold values from 0 to 15, all different within a row; in each aligned block of 256 rows (0 to 255, 256 to 511, ...) at most 48 rows name the same one
- gate_weight: bfloat16 [4096, 16], P('expert'), may hold values from -0.09375 to 0.09375
- expert_in: bfloat16 [16, 4096, 8192], P('dp', None, 'expert'), may hold values from -0.09375 to 0.09375
- expert_out: bfloat16 [16, 8192, 4096], P('dp', 'expert'), may hold values from -0.75 to 0.75
Outputs:
- mixed: bfloat16 [4096, 4096], P('dp', 'expert')
Inputs may be any that keep to these rules, and one draw needn't show every extreme that they name: `routing`: each row names two different experts. Within the 256 rows of one group, no expert is named by more than 48 rows, a bound that some block reaches.
All inputs are finite; a program needn't handle non-finite values.
Results may differ from a plain program's by a relative error of at most 0.02.
Values may be sent and summed in bfloat16 or wider, within the bound.
A program may use at most 64 MiB of HBM per device.

v0:
```python
import jax
import jax.numpy as jnp
from jax import lax
from jax.sharding import Mesh
from jax.sharding import PartitionSpec as P

EXPERT = ("expert_0", "expert_1")


def over_axes(value, axes):
    for axis in axes:
        value = lax.psum(value, axis)
    return value


def softmax_rows(logits):
    raised = jnp.exp(logits)
    return raised / jnp.sum(raised, axis=-1, keepdims=True)


def pick_chosen(softmax_all, picks):
    experts = softmax_all.shape[1]
    labels = lax.broadcasted_iota(jnp.int32, (picks.shape[0], 2, experts), 2)
    selected = labels == picks[:, :, None]
    return jnp.sum(jnp.where(selected, softmax_all[:, None, :], 0.0), axis=-1).astype(jnp.bfloat16)


def expert_rows(block_rows, weight_in, weight_out):
    sources = block_rows.shape[0]
    slots_here = block_rows.shape[1]
    width_local = block_rows.shape[2]
    flat_rows = block_rows.reshape(sources * slots_here, width_local)
    pre_act = jnp.dot(
        lax.all_gather(flat_rows, EXPERT, axis=1, tiled=True),
        weight_in,
        preferred_element_type=jnp.float32,
    )
    hidden = jax.nn.gelu(pre_act, approximate=True).astype(jnp.bfloat16)
    partial_out = jnp.dot(hidden, weight_out, preferred_element_type=jnp.float32)
    summed = lax.psum_scatter(
        partial_out.astype(jnp.bfloat16), EXPERT, scatter_dimension=1, tiled=True
    )
    return summed.reshape(sources, slots_here, width_local)


def shards(tokens, routing, gate_weight, expert_in, expert_out):
    group_size = tokens.shape[0]
    width_local = tokens.shape[1]
    experts = gate_weight.shape[1]
    dp_count = lax.axis_size("dp")
    capacity = 3 * group_size // dp_count
    weight_in = expert_in[0]
    weight_out = expert_out[0]
    partial_logits = jnp.dot(tokens, gate_weight, preferred_element_type=jnp.float32)
    logits = over_axes(partial_logits, EXPERT)
    chosen = pick_chosen(softmax_rows(logits), routing)
    order = jnp.concatenate([routing[:, 0], routing[:, 1]], axis=0)
    labels = lax.broadcasted_iota(jnp.int32, (2 * group_size, experts), 1)
    onehot = (labels == order[:, None]).astype(jnp.int32)
    before = jnp.cumsum(onehot, axis=0) - onehot
    slot_flat = jnp.sum(before * onehot, axis=1)
    slot_index = jnp.stack([slot_flat[:group_size], slot_flat[group_size:]], axis=1)
    target = routing * capacity + slot_index
    columns = lax.broadcasted_iota(jnp.int32, (group_size, experts * capacity), 1)
    first_hit = columns == target[:, 0:1]
    second_hit = columns == target[:, 1:2]
    assign = jnp.logical_or(first_hit, second_hit).astype(jnp.bfloat16)
    outgoing = jnp.einsum("gs,gd->sd", assign, tokens, preferred_element_type=jnp.float32)
    outgoing = outgoing.astype(jnp.bfloat16).reshape(experts, capacity, width_local)
    incoming = lax.all_to_all(outgoing, "dp", split_axis=0, concat_axis=0, tiled=True)
    processed = expert_rows(incoming, weight_in, weight_out)
    returned_rows = lax.all_to_all(processed, "dp", split_axis=0, concat_axis=0, tiled=True)
    zero_weight = jnp.zeros((), jnp.bfloat16)
    combine = jnp.where(first_hit, chosen[:, 0:1], zero_weight) + jnp.where(
        second_hit, chosen[:, 1:2], zero_weight
    )
    mixed = jnp.dot(
        combine,
        returned_rows.reshape(experts * capacity, width_local),
        preferred_element_type=jnp.float32,
    )
    return mixed.astype(jnp.bfloat16)


def solution(mesh):
    torus = Mesh(mesh.devices.reshape(mesh.shape["dp"], 8, 2), ("dp", "expert_0", "expert_1"))
    placed = (
        P("dp", EXPERT),
        P("dp", None),
        P(EXPERT, None),
        P("dp", None, EXPERT),
        P("dp", EXPERT, None),
    )
    return jax.shard_map(
        shards, mesh=torus, in_specs=placed, out_specs=P("dp", EXPERT), check_vma=False
    )
```

profile of v0, /device:TPU:1, one launch (start us, length us, event | category | flops | bytes accessed | tf_op | source)
XLA Modules:
  0.0 183.7 jit_solution(17316833488895113456)
XLA Ops:
  6.5 0.0 copy-start
  6.5 0.0 all-gather.2.cloned.1.call-start
  6.5 0.8 fusion.44
  7.3 1.2 reduce-window.6
  8.5 0.2 slice_reduce_fusion
  8.7 0.1 fusion.35
  8.9 0.7 add_add_fusion
  9.6 0.0 copy-done
  9.6 0.6 convolution_convert_fusion.1
  10.2 16.7 %all_to_all.10 = bf16[16,48,256]{2,1,0:T(8,128)(2,1)} all-to-all(bf16[16,48,256]{2,1,0:T(8,128)(2,1)S(1)} %bitcast.49), channel_id=1, replica_groups=mesh['dp'=16,'expert_0'=8,'expert_1'=2] {'dp'}, dimensions={0} | all-to-all | bytes 786432 | tf_op jit(solution)/shard_map/all_to_all | solution.py:70
  26.9 0.0 all-gather.2.cloned.1.call-update
  26.9 0.0 reduce-scatter.2.cloned.1.call-start
  26.9 57.6 %all-gather.2.cloned.1.call-done = bf16[768,4096]{1,0:T(8,128)(2,1)} async-done(((bf16[768,256]{1,0:T(8,128)(2,1)}), bf16[768,4096]{1,0:T(8,128)(2,1)}) %all-gather.2.cloned.1.call-update) | async-done | bytes 6291472 | tf_op jit(solution)/shard_map/all_gather | solution.py:34
  84.6 13.2 %convolution_convert_fusion = bf16[768,4096]{1,0:T(8,128)(2,1)} fusion(bf16[1,512,4096]{2,1,0:T(8,128)(2,1)} %param.9, bf16[768,4096]{1,0:T(8,128)(2,1)} %all-gather.2.cloned.1.call-done, bf16[1,4096,512]{2,1,0:T(8,128)(2,1)} %param.8), kind=kOutput, calls=%fused_computation | convolution fusion | flops 6449135616 | bytes 20971520 | tf_op jit(solution)/shard_map/dot_general | solution.py:39
  97.8 0.0 copy-start.2
  97.8 0.0 copy-start.1
  97.8 0.0 reduce-scatter.2.cloned.1.call-update
  97.8 0.7 copy-done.2
  98.5 0.1 fusion.45
  98.6 23.2 %psum.14 = f32[256,16]{0,1:T(8,128)S(1)} all-reduce(f32[256,16]{0,1:T(8,128)S(1)} %fusion.45), channel_id=1, replica_groups=mesh['dp'=16,'expert_0'=8,'expert_1'=2] {'expert_0'}, use_global_device_ids=true, to_apply=%region_3.4 | all-reduce | flops 4096 | bytes 32768 | tf_op jit(solution)/shard_map/psum | solution.py:12
  121.9 10.1 %psum.15 = f32[256,16]{0,1:T(8,128)S(1)} all-reduce(f32[256,16]{0,1:T(8,128)S(1)} %psum.14), channel_id=1, replica_groups=mesh['dp'=16,'expert_0'=8,'expert_1'=2] {'expert_1'}, use_global_device_ids=true, to_apply=%region_4.5 | all-reduce | flops 4096 | bytes 32768 | tf_op jit(solution)/shard_map/psum | solution.py:12
  132.0 28.9 %reduce-scatter.2.cloned.1.call-done = bf16[768,256]{1,0:T(8,128)(2,1)} async-done(((bf16[768,4096]{1,0:T(8,128)(2,1)}), bf16[768,256]{1,0:T(8,128)(2,1)}) %reduce-scatter.2.cloned.1.call-update) | async-done | bytes 393232 | tf_op jit(solution)/shard_map/reduce_scatter | solution.py:40
  160.9 6.6 %all-to-all-start.1 = ((bf16[16,48,256]{2,1,0:T(8,128)(2,1)}), bf16[16,48,256]{2,1,0:T(8,128)(2,1)S(1)}, u32[]{:S(2)}, u32[]{:S(2)}) async-start(bf16[16,48,256]{2,1,0:T(8,128)(2,1)} %bitcast.47), calls=%async_computation.2 | async-start | bytes 786432 | tf_op jit(solution)/shard_map/all_to_all | solution.py:72
  167.5 0.0 copy-done.1
  167.6 8.2 %all-to-all-done.1 = bf16[16,48,256]{2,1,0:T(8,128)(2,1)S(1)} async-done(((bf16[16,48,256]{2,1,0:T(8,128)(2,1)}), bf16[16,48,256]{2,1,0:T(8,128)(2,1)S(1)}, u32[]{:S(2)}, u32[]{:S(2)}) %all-to-all-start.1) | async-done | bytes 393248 | tf_op jit(solution)/shard_map/all_to_all | solution.py:72
  175.8 1.0 convolution_convert_fusion.2
  (11 shorter events, 0.2 us)
Async XLA Ops:
  6.5 3.0 %copy-start = (bf16[256,256]{1,0:T(8,128)(2,1)S(1)}, bf16[256,256]{1,0:T(8,128)(2,1)}, u32[]{:S(2)}) copy-start(bf16[256,256]{1,0:T(8,128)(2,1)} %param.5) | copy-start | bytes 393220
  6.5 78.0 %all-gather.2.cloned.1.call-start = ((), (), s32[]{:S(2)}) async-start(), calls=%async_computation.3 | async-start | bytes 6684672 | tf_op jit(solution)/shard_map/all_gather | solution.py:34
  26.9 134.0 %reduce-scatter.2.cloned.1.call-start = ((), (), s32[]{:S(2)}) async-start(), calls=%async_computation.4 | async-start | bytes 6684672 | tf_op jit(solution)/shard_map/reduce_scatter | solution.py:40
  97.8 0.7 copy-start.2
  97.8 69.8 %copy-start.1 = (s32[256,2]{0,1:T(2,128)S(1)}, s32[256,2]{0,1:T(2,128)}, u32[]{:S(2)}) copy-start(s32[256,2]{0,1:T(2,128)} %param.6) | copy-start | bytes 6148
  160.9 14.9 %all-to-all-start.1 = ((bf16[16,48,256]{2,1,0:T(8,128)(2,1)}), bf16[16,48,256]{2,1,0:T(8,128)(2,1)S(1)}, u32[]{:S(2)}, u32[]{:S(2)}) async-start(bf16[16,48,256]{2,1,0:T(8,128)(2,1)} %bitcast.47), calls=%async_computation.2 | async-start | bytes 786432 | tf_op jit(solution)/shard_map/all_to_all | solution.py:72
Sparse Core Ops, SparseCore 0:
  27.0 57.5 all-gather.1
  97.9 62.8 reduce-scatter.1
where the time goes:
time: 187 us; the launch traced here: 184 us
  waiting for transfers between devices  94.8 us (51%)
  blocking collectives  50 us (27%)
  matrix products  15 us (8%)
  between operations  13.5 us (7%)
  starting transfers between devices  6.69 us (4%)
  other arithmetic  2.06 us (1%)
    all_gather x1, waiting for transfers between devices, expert_rows(): lax.all_gather(flat_rows, EXPERT, axis=1, tiled=True)  57.6 us
    psum x2, blocking collectives, over_axes(): value = lax.psum(value, axis)  33.3 us
    reduce_scatter x1, waiting for transfers between devices, expert_rows(): lax.psum_scatter(partial_out.astype(jnp.bfloat16), EXPERT, scatter_dimens...  28.9 us
    all_to_all x1, blocking collectives, shards(): lax.all_to_all(outgoing, 'dp', split_axis=0, concat_axis=0, tiled=True)  16.7 us
    dot_general x1, matrix products, expert_rows(): jnp.dot(hidden, weight_out, preferred_element_type=jnp.float32)  13.2 us
    all_to_all x1, waiting for transfers between devices, shards(): lax.all_to_all(processed, 'dp', split_axis=0, concat_axis=0, tiled=True)  8.18 us
    all_to_all x1, starting transfers between devices, shards(): lax.all_to_all(processed, 'dp', split_axis=0, concat_axis=0, tiled=True)  6.64 us
  transfers between devices with their start and end apart: 3, of which 3 were waited for; matrix products, arithmetic and copies ran while one was open for 0% of the time, Pallas kernels for 0%

commit v1 on v0

v1 whole, which is shorter than its diff:
```python
import functools

import jax
import jax.numpy as jnp
from jax import lax
from jax.experimental import pallas as pl
from jax.experimental.pallas import tpu as pltpu
from jax.sharding import PartitionSpec as P

MESH = pl.DeviceIdType.MESH
F32 = jnp.float32
BF16 = jnp.bfloat16

X, Y, Z = 4, 4, 8
GROUP, CAP, EXPERTS, W, HID = 256, 48, 16, 256, 512
SHIFTS = [(dx, dy) for dy in (-1, 0, 1) for dx in (-1, 0, 1)]
SHIFTS += [(2, dy) for dy in (-1, 0, 1, 2)] + [(dx, 2) for dx in (-1, 0, 1)]
NEAR, FAR, SELF = 9, 7, 4
NR, FR = NEAR * CAP, FAR * CAP
NEAR_ORDER = [1, 3, 7, 5, 0, 8, 2, 6]
FAR_ORDER = [12, 9, 11, 13, 15, 10, 14]
TB = GROUP + EXPERTS
T_HALF = ((0, 128), (128, TB - 128))
F_HALF = ((0, 192), (192, FR - 192))
M_HALF = ((0, 128), (128, 128))


def parts_of(step):
    return ((0, 0), (1, 1)) if step == 4 else ((0, 0), (1, 1), (0, 1), (1, 0))


def back_parts_of(step):
    return ((0, 0), (1, 1)) if step == 1 else ((0, 0), (1, 1), (0, 1), (1, 0))


def offset_of(slot):
    return 4 if slot == 7 else (slot // 2 if slot % 2 == 0 else -((slot + 1) // 2))


def gather_slots(step, way):
    source = 0 if step == 1 else 2 * step - 3 + way
    return source, (7 if step == 4 else 2 * step - 1 + way)


def back_slot(step, way):
    return 7 if step == 1 else 2 * (5 - step) - way


def kernel(
    tokens, routing, gate, w_in, w_out, out,
    tg, assign, near_send, far_send, xn, xf, acc_n, acc_f, w1, w2, hn, hf,
    pf, rf, pn, rn, pm, rm, fr, ra, cn, cf, lg, lg_other, base,
    tok_sem, w1_sem, w2_sem, w2s_send, w2s_recv,
    f1_send, f1_recv, a1_send, a1_recv, f2_send, f2_recv, a2_send, a2_recv,
    sn_send, sn_recv, sf_send, sf_recv, h_send, h_recv, l_send, l_recv,
    bf_send, bf_recv, bn_send, bn_recv, bm_send, bm_recv, ra_send, ra_recv,
):
    dp = lax.axis_index("dp")
    ex = lax.axis_index("expert")
    gy, gx = lax.div(dp, X), lax.rem(dp, X)
    z, core = lax.div(ex, 2), lax.rem(ex, 2)

    def plane(dx, dy):
        return (lax.rem(gy + dy + Y, Y) * X + lax.rem(gx + dx + X, X), ex)

    def ring(offset):
        return lax.rem(z + offset + Z, Z)

    to = [plane(dx, dy) for dx, dy in SHIFTS]
    back = [plane(-dx, -dy) for dx, dy in SHIFTS]
    along = ((dp, ring(1) * 2 + core), (dp, ring(-1) * 2 + core))
    sibling = (dp, z * 2 + 1 - core)

    def remote(src, dst, send, recv, device):
        return pltpu.make_async_remote_copy(
            src_ref=src, dst_ref=dst, send_sem=send, recv_sem=recv,
            device_id=device, device_id_type=MESH,
        )

    barrier = pltpu.get_barrier_semaphore()
    for device in [to[p] for p in range(EXPERTS) if p != SELF] + [*along, sibling]:
        pl.semaphore_signal(barrier, inc=1, device_id=device, device_id_type=MESH)

    token_copy = pltpu.make_async_copy(tokens, tg.at[0, pl.ds(0, GROUP)], tok_sem)
    token_copy.start()
    tg[0, GROUP:TB, :] = gate[...]

    def w1_copy(slot, side):
        rows = (ring(offset_of(slot)) * 2 + (core if side == 0 else 1 - core)) * W
        return pltpu.make_async_copy(
            w_in.at[0, pl.ds(pl.multiple_of(rows, W), W), :], w1.at[slot, side], w1_sem.at[slot, side]
        )

    def w2_columns(slot, side):
        columns = (ring(offset_of(slot)) * 2 + (core if side == 0 else 1 - core)) * W
        return w_out.at[0, :, pl.ds(pl.multiple_of(columns, W), W)]

    def w2_copy(slot):
        return pltpu.make_async_copy(w2_columns(slot, 0), w2.at[slot, pl.ds(0, HID)], w2_sem.at[slot])

    def w2_share(slot):
        return remote(
            w2_columns(slot, 1), w2.at[slot, pl.ds(HID, HID)], w2s_send.at[slot], w2s_recv.at[slot], sibling
        )

    for slot in range(Z):
        for side in range(2):
            w1_copy(slot, side).start()
    for slot in range(Z):
        w2_copy(slot).start()

    names = lax.broadcasted_iota(jnp.int32, (EXPERTS, GROUP), 0)
    sx = (lax.rem(names, X) - gx + 1 + X) & 3
    sy = (lax.div(names, X) - gy + 1 + Y) & 3
    place = jnp.where(sx == 3, NEAR + sy, jnp.where(sy == 3, 13 + sx, sy * 3 + sx))
    place = (place * CAP).astype(F32)
    first = (names == routing[0:1, :]).astype(F32)
    second = (names == routing[1:2, :]).astype(F32)
    earlier = lax.broadcasted_iota(jnp.int32, (GROUP, GROUP), 0)
    later = lax.broadcasted_iota(jnp.int32, (GROUP, GROUP), 1)
    upper = (earlier < later).astype(F32).astype(BF16)
    before_first = jnp.dot(first.astype(BF16), upper, preferred_element_type=F32)
    before_second = jnp.dot(second.astype(BF16), upper, preferred_element_type=F32)
    before_second = before_second + jnp.sum(first, axis=1, keepdims=True)
    row_first = jnp.sum(first * (place + before_first), axis=0, keepdims=True)
    row_second = jnp.sum(second * (place + before_second), axis=0, keepdims=True)
    rows = lax.broadcasted_iota(jnp.int32, (EXPERTS * CAP, GROUP), 0)
    hit = (rows == row_first.astype(jnp.int32)) | (rows == row_second.astype(jnp.int32))
    assign[...] = hit.astype(F32).astype(BF16)
    base[0:1, :] = row_first
    base[1:2, :] = row_second
    lg[...] = jnp.zeros_like(lg)

    token_copy.wait()
    far_send[...] = jnp.dot(
        assign[NR:, :], tg[0, 0:GROUP, :], preferred_element_type=F32
    ).astype(BF16)

    def dispatch_near(slot):
        rows_of = jnp.dot(assign[0:NR, :], tg[slot, 0:GROUP, :], preferred_element_type=F32).astype(BF16)
        near_send[slot] = rows_of
        xn[slot, 0, SELF * CAP:(SELF + 1) * CAP, :] = rows_of[SELF * CAP:(SELF + 1) * CAP, :]
        lg[...] += lax.dot_general(
            tg[slot, GROUP:TB, :], tg[slot, 0:GROUP, :], (((1,), (1,)), ((), ())), preferred_element_type=F32
        )

    dispatch_near(0)

    pl.semaphore_wait(barrier, 18)

    def f1(step, way, half):
        source, target = gather_slots(step, way)
        start, size = T_HALF[half]
        return remote(
            tg.at[source, pl.ds(start, size)], tg.at[target, pl.ds(start, size)],
            f1_send.at[step - 1, way, half], f1_recv.at[step - 1, way, half], along[way],
        )

    def a1(p):
        block = pl.ds((p - NEAR) * CAP, CAP)
        return remote(far_send.at[block], xf.at[0, 0, block], a1_send, a1_recv, to[p])

    def f2(slot, p):
        block = pl.ds(p * CAP, CAP)
        return remote(
            near_send.at[slot, block], xn.at[slot, 0, block], f2_send.at[slot], f2_recv.at[slot], to[p]
        )

    def f2_all(slot):
        block = pl.ds(0, NR - CAP)
        return remote(
            near_send.at[slot, block], xn.at[slot, 0, block], f2_send.at[slot], f2_recv.at[slot], sibling
        )

    def a2(step, way, half):
        source, target = gather_slots(step, way)
        start, size = F_HALF[half]
        return remote(
            xf.at[source, 0, pl.ds(start, size)], xf.at[target, 0, pl.ds(start, size)],
            a2_send.at[step - 1, way, half], a2_recv.at[step - 1, way, half], along[way],
        )

    def share_near(slot):
        return remote(xn.at[slot, 0], xn.at[slot, 1], sn_send.at[slot], sn_recv.at[slot], sibling)

    def share_far(slot):
        return remote(xf.at[slot, 0], xf.at[slot, 1], sf_send.at[slot], sf_recv.at[slot], sibling)

    def send_near(slot):
        for p in NEAR_ORDER:
            f2(slot, p).start()

    def pass_on(transfer, step):
        for way, half in parts_of(step):
            transfer(step, way, half).wait_recv()
            if step < 4 and (way, half) in parts_of(step + 1):
                transfer(step + 1, way, half).start()

    for way, half in parts_of(1):
        f1(1, way, half).start()
    for p in FAR_ORDER:
        a1(p).start()
    send_near(0)

    acc_n[...] = jnp.zeros_like(acc_n)
    acc_f[...] = jnp.zeros_like(acc_f)

    def both(lower, upper, work):
        lax.fori_loop(lower, upper, lambda slot, carry: (work(slot), carry)[1], 0)

    def near_part(slot):
        dispatch_near(slot)
        send_near(slot)

    def multiply(rows_of, total, side):
        def work(slot):
            total[...] += jnp.dot(rows_of[slot, side], w1[slot, side], preferred_element_type=F32)

        return work

    def near_in(slot):
        f2_all(slot).wait_recv()
        share_near(slot).start()

    def near_multiply(slot):
        multiply(xn, acc_n, 0)(slot)
        share_near(slot).wait_recv()
        multiply(xn, acc_n, 1)(slot)

    def far_multiply(slot):
        multiply(xf, acc_f, 0)(slot)
        share_far(slot).wait_recv()
        multiply(xf, acc_f, 1)(slot)

    pass_on(f1, 1)
    both(1, 3, near_part)
    pl_all = pl.ds(0, FR)
    remote(far_send.at[pl_all], xf.at[0, 0, pl_all], a1_send, a1_recv, sibling).wait_recv()
    for way, half in parts_of(1):
        a2(1, way, half).start()
    share_far(0).start()
    pass_on(f1, 2)
    both(3, 5, near_part)
    near_in(0)
    pass_on(a2, 1)
    share_far(1).start()
    share_far(2).start()
    pass_on(f1, 3)
    both(5, 7, near_part)
    for slot in range(Z):
        w2_share(slot).start()
    for slot in range(Z):
        for side in range(2):
            w1_copy(slot, side).wait()
    both(1, 3, near_in)
    pass_on(f1, 4)
    both(7, 8, near_part)

    logit_copy = remote(lg, lg_other, l_send, l_recv, sibling)
    logit_copy.start()
    pass_on(a2, 2)
    share_far(3).start()
    share_far(4).start()

    def first_multiplies(slot):
        near_multiply(slot)
        far_multiply(slot)

    both(0, 3, first_multiplies)
    both(3, 7, near_in)
    pass_on(a2, 3)
    share_far(5).start()
    share_far(6).start()
    both(3, 7, near_multiply)
    near_in(7)

    logit_copy.wait()
    raised = jnp.exp(lg[...] + lg_other[...])
    probs = raised / jnp.sum(raised, axis=0, keepdims=True)
    chosen_first = jnp.sum(jnp.where(names == routing[0:1, :], probs, 0.0), axis=0, keepdims=True)
    chosen_second = jnp.sum(jnp.where(names == routing[1:2, :], probs, 0.0), axis=0, keepdims=True)
    packed = jnp.concatenate(
        [base[0:1, :], base[1:2, :], chosen_first, chosen_second, jnp.zeros((124, GROUP), F32)], axis=0
    )
    packed = jnp.transpose(packed)
    at_first, at_second = packed[:, 0:1].astype(jnp.int32), packed[:, 1:2].astype(jnp.int32)
    by_first, by_second = packed[:, 2:3], packed[:, 3:4]

    def weights(start, size):
        columns = lax.broadcasted_iota(jnp.int32, (GROUP, size), 1) + start
        return (
            jnp.where(columns == at_first, by_first, 0.0) + jnp.where(columns == at_second, by_second, 0.0)
        ).astype(BF16)

    cn[...] = weights(0, NR)
    cf[...] = weights(NR, FR)

    both(7, 8, near_multiply)

    def share_hidden(buffer, which):
        return remote(
            buffer.at[0], buffer.at[1], h_send.at[which], h_recv.at[which], sibling
        )

    hn[0] = jax.nn.gelu(acc_n[...], approximate=True).astype(BF16)
    share_hidden(hn, 0).start()
    pass_on(a2, 4)
    share_far(7).start()
    both(3, 7, far_multiply)
    for slot in range(Z):
        w2_copy(slot).wait()
        w2_share(slot).wait_recv()

    def bn(slot, p):
        block = pl.ds(p * CAP, CAP)
        return remote(
            pn.at[slot, block], rn.at[slot, block], bn_send.at[slot], bn_recv.at[slot], back[p]
        )

    def bn_all(slot):
        block = pl.ds(0, NR - CAP)
        return remote(
            pn.at[slot, block], rn.at[slot, block], bn_send.at[slot], bn_recv.at[slot], sibling
        )

    def second(buffer, slot):
        return (
            jnp.dot(buffer[0], w2[slot, 0:HID, :], preferred_element_type=F32)
            + jnp.dot(buffer[1], w2[slot, HID:2 * HID, :], preferred_element_type=F32)
        ).astype(BF16)

    def near_out(index):
        slot = 7 - index
        terms = second(hn, slot)
        pn[slot] = terms
        rn[slot, SELF * CAP:(SELF + 1) * CAP, :] = terms[SELF * CAP:(SELF + 1) * CAP, :]
        for p in NEAR_ORDER:
            bn(slot, p).start()

    share_hidden(hn, 0).wait_recv()
    both(0, 4, near_out)
    both(7, 8, far_multiply)
    hf[0] = jax.nn.gelu(acc_f[...], approximate=True).astype(BF16)
    share_hidden(hf, 1).start()
    both(4, 8, near_out)
    share_hidden(hf, 1).wait_recv()

    def far_out(index):
        slot = 7 - index
        pf[slot] = second(hf, slot)

    def reduce_copy(own, received, halves, send, recv, step, way, half):
        start, size = halves[half]
        return remote(
            own.at[back_slot(step, way), pl.ds(start, size)], received.at[way, step - 1, pl.ds(start, size)],
            send.at[step - 1, way, half], recv.at[step - 1, way, half], along[way],
        )

    bf = functools.partial(reduce_copy, pf, rf, F_HALF, bf_send, bf_recv)
    bm = functools.partial(reduce_copy, pm, rm, M_HALF, bm_send, bm_recv)

    def reduce_step(transfer, own, received, halves, step):
        for way, half in back_parts_of(step):
            if step > 1 and (way, half) in back_parts_of(step - 1):
                transfer(step - 1, way, half).wait_recv()
                start, size = halves[half]
                slot = back_slot(step, way)
                own[slot, start:start + size, :] = (
                    own[slot, start:start + size, :].astype(F32)
                    + received[way, step - 2, start:start + size, :].astype(F32)
                ).astype(BF16)
            transfer(step, way, half).start()

    def mix(slot):
        bn_all(slot).wait_recv()
        pm[slot] = jnp.dot(cn[...], rn[slot], preferred_element_type=F32).astype(BF16)

    def mix_down(index):
        mix(7 - index)

    both(0, 1, far_out)
    reduce_step(bf, pf, rf, F_HALF, 1)
    both(1, 3, far_out)
    both(0, 1, mix_down)
    reduce_step(bm, pm, rm, M_HALF, 1)
    both(3, 8, far_out)
    reduce_step(bf, pf, rf, F_HALF, 2)
    both(1, 3, mix_down)
    reduce_step(bm, pm, rm, M_HALF, 2)
    both(3, 5, mix_down)
    reduce_step(bf, pf, rf, F_HALF, 3)
    reduce_step(bm, pm, rm, M_HALF, 3)
    both(5, 8, mix_down)
    reduce_step(bf, pf, rf, F_HALF, 4)
    reduce_step(bm, pm, rm, M_HALF, 4)

    for way, half in back_parts_of(4):
        bf(4, way, half).wait_recv()
    fr[...] = (
        pf[0].astype(F32) + rf[0, 3].astype(F32) + rf[1, 3].astype(F32)
    ).astype(BF16)

    def far_back(p):
        block = pl.ds((p - NEAR) * CAP, CAP)
        return remote(fr.at[block], ra.at[block], ra_send, ra_recv, back[p])

    for p in FAR_ORDER:
        far_back(p).start()
    for way, half in back_parts_of(4):
        bm(4, way, half).wait_recv()
    partial = pm[0].astype(F32) + rm[0, 3].astype(F32) + rm[1, 3].astype(F32)
    remote(fr, ra, ra_send, ra_recv, sibling).wait_recv()
    out[...] = (partial + jnp.dot(cf[...], ra[...], preferred_element_type=F32)).astype(BF16)

    for step in range(1, 5):
        for way, half in parts_of(step):
            f1(step, way, half).wait_send()
            a2(step, way, half).wait_send()
        for way, half in back_parts_of(step):
            bf(step, way, half).wait_send()
            bm(step, way, half).wait_send()
    remote(far_send.at[pl_all], xf.at[0, 0, pl_all], a1_send, a1_recv, sibling).wait_send()
    remote(fr, ra, ra_send, ra_recv, sibling).wait_send()

    def sent(slot):
        f2_all(slot).wait_send()
        bn_all(slot).wait_send()
        share_near(slot).wait_send()
        share_far(slot).wait_send()

    both(0, Z, sent)
    for slot in range(Z):
        w2_share(slot).wait_send()
    share_hidden(hn, 0).wait_send()
    share_hidden(hf, 1).wait_send()


def layer(tokens, routing, gate_weight, expert_in, expert_out):
    vmem = pl.BlockSpec(memory_space=pltpu.VMEM)
    anywhere = pl.BlockSpec(memory_space=pl.ANY)
    dma = pltpu.SemaphoreType.DMA
    return pl.pallas_call(
        kernel,
        out_shape=jax.ShapeDtypeStruct((GROUP, W), BF16),
        in_specs=[anywhere, vmem, vmem, anywhere, anywhere],
        out_specs=vmem,
        scratch_shapes=[
            pltpu.VMEM((Z, TB, W), BF16),
            pltpu.VMEM((EXPERTS * CAP, GROUP), BF16),
            pltpu.VMEM((Z, NR, W), BF16),
            pltpu.VMEM((FR, W), BF16),
            pltpu.VMEM((Z, 2, NR, W), BF16),
            pltpu.VMEM((Z, 2, FR, W), BF16),
            pltpu.VMEM((NR, HID), F32),
            pltpu.VMEM((FR, HID), F32),
            pltpu.VMEM((Z, 2, W, HID), BF16),
            pltpu.VMEM((Z, 2 * HID, W), BF16),
            pltpu.VMEM((2, NR, HID), BF16),
            pltpu.VMEM((2, FR, HID), BF16),
            pltpu.VMEM((Z, FR, W), BF16),
            pltpu.VMEM((2, 4, FR, W), BF16),
            pltpu.VMEM((Z, NR, W), BF16),
            pltpu.VMEM((Z, NR, W), BF16),
            pltpu.VMEM((Z, GROUP, W), BF16),
            pltpu.VMEM((2, 4, GROUP, W), BF16),
            pltpu.VMEM((FR, W), BF16),
            pltpu.VMEM((FR, W), BF16),
            pltpu.VMEM((GROUP, NR), BF16),
            pltpu.VMEM((GROUP, FR), BF16),
            pltpu.VMEM((EXPERTS, GROUP), F32),
            pltpu.VMEM((EXPERTS, GROUP), F32),
            pltpu.VMEM((8, GROUP), F32),
            dma, dma((Z, 2)), dma((Z,)), dma((Z,)), dma((Z,)),
            dma((4, 2, 2)), dma((4, 2, 2)), dma, dma, dma((Z,)), dma((Z,)), dma((4, 2, 2)), dma((4, 2, 2)),
            dma((Z,)), dma((Z,)), dma((Z,)), dma((Z,)), dma((2,)), dma((2,)), dma, dma,
            dma((4, 2, 2)), dma((4, 2, 2)), dma((Z,)), dma((Z,)), dma((4, 2, 2)), dma((4, 2, 2)), dma, dma,
        ],
        compiler_params=pltpu.CompilerParams(collective_id=0, has_side_effects=True),
        name="experts",
    )(tokens, routing.T, gate_weight.T, expert_in, expert_out)


def solution(mesh):
    return jax.shard_map(
        layer,
        mesh=mesh,
        in_specs=(
            P("dp", "expert"),
            P("dp", None),
            P("expert", None),
            P("dp", None, "expert"),
            P("dp", "expert", None),
        ),
        out_specs=P("dp", "expert"),
        check_vma=False,
    )
```

time: 187 us -> 79.5 us (0.43)
  the two profiles are of different devices: /device:TPU:1 before, /device:TPU:8 now
where the time goes in v1:
time: 79.5 us; the launch traced here: 79.3 us
  Pallas kernels  77.8 us (98%)
  local copies, waits for them, and re-layouts  1.57 us (2%)
    pallas_call x1, Pallas kernels, layer(): pl.pallas_call(kernel, out_shape=jax.ShapeDtypeStruct((GROUP, W), BF16),...  77.8 us

profile of v1, /device:TPU:8, one launch (start us, length us, event | category | flops | bytes accessed | tf_op | source)
XLA Modules:
  0.0 79.3 jit_solution(11958706667060194955)
XLA Ops:
  0.0 77.8 %experts.1 = bf16[256,256]{1,0:T(8,128)(2,1)} custom-call(bf16[256,256]{1,0:T(8,128)(2,1)} %tokens.1, s32[2,256]{1,0:T(2,128)} %bitcast.3, bf16[16,256]{1,0:T(8,128)(2,1)} %bitcast.2, bf16[1,4096,512]{2,1,0:T(8,128)(2,1)} %w_in.1, bf16[1,512,4096]{2,1,0:T(8,128)(2,1)} %w_out.1), custom_call_target="tpu_custom_call" | custom-call | tf_op jit(solution)/shard_map/experts/pallas_call | solution.py:442
  77.8 1.6 %copy.7 = bf16[256,256]{1,0:T(8,128)(2,1)} copy(bf16[256,256]{1,0:T(8,128)(2,1)} %experts.1) | data formatting | bytes 262144

commit v2 on v1

--- a/solution.py
+++ b/solution.py
@@ -14,14 +14,14 @@
 X, Y, Z = 4, 4, 8
 GROUP, CAP, EXPERTS, W, HID = 256, 48, 16, 256, 512
 SHIFTS = [(dx, dy) for dy in (-1, 0, 1) for dx in (-1, 0, 1)]
-SHIFTS += [(2, dy) for dy in (-1, 0, 1, 2)] + [(dx, 2) for dx in (-1, 0, 1)]
-NEAR, FAR, SELF = 9, 7, 4
+SHIFTS += [(2, 0), (0, 2), (2, -1), (2, 1), (2, 2), (-1, 2), (1, 2)]
+NEAR, FAR, SELF = 11, 5, 4
 NR, FR = NEAR * CAP, FAR * CAP
-NEAR_ORDER = [1, 3, 7, 5, 0, 8, 2, 6]
-FAR_ORDER = [12, 9, 11, 13, 15, 10, 14]
+NEAR_ORDER = [1, 3, 7, 5, 9, 10, 0, 8, 2, 6]
+FAR_ORDER = [13, 11, 14, 12, 15]
 TB = GROUP + EXPERTS
 T_HALF = ((0, 128), (128, TB - 128))
-F_HALF = ((0, 192), (192, FR - 192))
+F_HALF = ((0, 3 * CAP), (3 * CAP, FR - 3 * CAP))
 M_HALF = ((0, 128), (128, 128))
 
 
@@ -49,7 +49,7 @@
 def kernel(
     tokens, routing, gate, w_in, w_out, out,
     tg, assign, near_send, far_send, xn, xf, acc_n, acc_f, w1, w2, hn, hf,
-    pf, rf, pn, rn, pm, rm, fr, ra, cn, cf, lg, lg_other, base,
+    pf, rf, pn, rn, pm, rm, fr, ra, cn, cf, lg, lg_other, base, far_term,
     tok_sem, w1_sem, w2_sem, w2s_send, w2s_recv,
     f1_send, f1_recv, a1_send, a1_recv, f2_send, f2_recv, a2_send, a2_recv,
     sn_send, sn_recv, sf_send, sf_recv, h_send, h_recv, l_send, l_recv,
@@ -103,16 +103,61 @@
             w2_columns(slot, 1), w2.at[slot, pl.ds(HID, HID)], w2s_send.at[slot], w2s_recv.at[slot], sibling
         )
 
-    for slot in range(Z):
-        for side in range(2):
-            w1_copy(slot, side).start()
-    for slot in range(Z):
-        w2_copy(slot).start()
+    def f1(step, way, half):
+        source, target = gather_slots(step, way)
+        start, size = T_HALF[half]
+        return remote(
+            tg.at[source, pl.ds(start, size)], tg.at[target, pl.ds(start, size)],
+            f1_send.at[step - 1, way, half], f1_recv.at[step - 1, way, half], along[way],
+        )
+
+    def a1(p):
+        block = pl.ds((p - NEAR) * CAP, CAP)
+        return remote(far_send.at[block], xf.at[0, 0, block], a1_send, a1_recv, to[p])
+
+    def f2(slot, p):
+        block = pl.ds(p * CAP, CAP)
+        return remote(
+            near_send.at[slot, block], xn.at[slot, 0, block], f2_send.at[slot], f2_recv.at[slot], to[p]
+        )
+
+    def f2_all(slot):
+        block = pl.ds(0, NR - CAP)
+        return remote(
+            near_send.at[slot, block], xn.at[slot, 0, block], f2_send.at[slot], f2_recv.at[slot], sibling
+        )
+
+    def a2(step, way, half):
+        source, target = gather_slots(step, way)
+        start, size = F_HALF[half]
+        return remote(
+            xf.at[source, 0, pl.ds(start, size)], xf.at[target, 0, pl.ds(start, size)],
+            a2_send.at[step - 1, way, half], a2_recv.at[step - 1, way, half], along[way],
+        )
+
+    def share_near(slot):
+        return remote(xn.at[slot, 0], xn.at[slot, 1], sn_send.at[slot], sn_recv.at[slot], sibling)
+
+    def share_far(slot):
+        return remote(xf.at[slot, 0], xf.at[slot, 1], sf_send.at[slot], sf_recv.at[slot], sibling)
+
+    def send_near(slot):
+        for p in NEAR_ORDER:
+            f2(slot, p).start()
+
+    def pass_on(transfer, step):
+        for way, half in parts_of(step):
+            transfer(step, way, half).wait_recv()
+            if step < 4 and (way, half) in parts_of(step + 1):
+                transfer(step + 1, way, half).start()
 
     names = lax.broadcasted_iota(jnp.int32, (EXPERTS, GROUP), 0)
     sx = (lax.rem(names, X) - gx + 1 + X) & 3
     sy = (lax.div(names, X) - gy + 1 + Y) & 3
-    place = jnp.where(sx == 3, NEAR + sy, jnp.where(sy == 3, 13 + sx, sy * 3 + sx))
+    place = sy * 3 + sx
+    for p in range(9, EXPERTS):
+        dx, dy = SHIFTS[p]
+        place = jnp.where((sx == dx + 1) & (sy == dy + 1), p, place)
     place = (place * CAP).astype(F32)
     first = (names == routing[0:1, :]).astype(F32)
     second = (names == routing[1:2, :]).astype(F32)
@@ -132,6 +177,9 @@
     lg[...] = jnp.zeros_like(lg)
 
     token_copy.wait()
+    pl.semaphore_wait(barrier, 18)
+    for way, half in parts_of(1):
+        f1(1, way, half).start()
     far_send[...] = jnp.dot(
         assign[NR:, :], tg[0, 0:GROUP, :], preferred_element_type=F32
     ).astype(BF16)
@@ -144,63 +192,15 @@
             tg[slot, GROUP:TB, :], tg[slot, 0:GROUP, :], (((1,), (1,)), ((), ())), preferred_element_type=F32
         )
 
-    dispatch_near(0)
-
-    pl.semaphore_wait(barrier, 18)
-
-    def f1(step, way, half):
-        source, target = gather_slots(step, way)
-        start, size = T_HALF[half]
-        return remote(
-            tg.at[source, pl.ds(start, size)], tg.at[target, pl.ds(start, size)],
-            f1_send.at[step - 1, way, half], f1_recv.at[step - 1, way, half], along[way],
-        )
-
-    def a1(p):
-        block = pl.ds((p - NEAR) * CAP, CAP)
-        return remote(far_send.at[block], xf.at[0, 0, block], a1_send, a1_recv, to[p])
-
-    def f2(slot, p):
-        block = pl.ds(p * CAP, CAP)
-        return remote(
-            near_send.at[slot, block], xn.at[slot, 0, block], f2_send.at[slot], f2_recv.at[slot], to[p]
-        )
-
-    def f2_all(slot):
-        block = pl.ds(0, NR - CAP)
-        return remote(
-            near_send.at[slot, block], xn.at[slot, 0, block], f2_send.at[slot], f2_recv.at[slot], sibling
-        )
-
-    def a2(step, way, half):
-        source, target = gather_slots(step, way)
-        start, size = F_HALF[half]
-        return remote(
-            xf.at[source, 0, pl.ds(start, size)], xf.at[target, 0, pl.ds(start, size)],
-            a2_send.at[step - 1, way, half], a2_recv.at[step - 1, way, half], along[way],
-        )
-
-    def share_near(slot):
-        return remote(xn.at[slot, 0], xn.at[slot, 1], sn_send.at[slot], sn_recv.at[slot], sibling)
-
-    def share_far(slot):
-        return remote(xf.at[slot, 0], xf.at[slot, 1], sf_send.at[slot], sf_recv.at[slot], sibling)
-
-    def send_near(slot):
-        for p in NEAR_ORDER:
-            f2(slot, p).start()
-
-    def pass_on(transfer, step):
-        for way, half in parts_of(step):
-            transfer(step, way, half).wait_recv()
-            if step < 4 and (way, half) in parts_of(step + 1):
-                transfer(step + 1, way, half).start()
-
-    for way, half in parts_of(1):
-        f1(1, way, half).start()
     for p in FAR_ORDER:
         a1(p).start()
+    dispatch_near(0)
     send_near(0)
+    for slot in range(Z):
+        for side in range(2):
+            w1_copy(slot, side).start()
+    for slot in range(Z):
+        w2_copy(slot).start()
 
     acc_n[...] = jnp.zeros_like(acc_n)
     acc_f[...] = jnp.zeros_like(acc_f)
@@ -242,17 +242,21 @@
     pass_on(f1, 2)
     both(3, 5, near_part)
     near_in(0)
+    for slot in range(Z):
+        for side in range(2):
+            w1_copy(slot, side).wait()
+    both(0, 1, far_multiply)
     pass_on(a2, 1)
     share_far(1).start()
     share_far(2).start()
+    both(0, 1, near_multiply)
     pass_on(f1, 3)
     both(5, 7, near_part)
+    both(1, 3, near_in)
     for slot in range(Z):
         w2_share(slot).start()
-    for slot in range(Z):
-        for side in range(2):
-            w1_copy(slot, side).wait()
-    both(1, 3, near_in)
+    both(1, 3, far_multiply)
+    both(1, 2, near_multiply)
     pass_on(f1, 4)
     both(7, 8, near_part)
 
@@ -261,18 +265,14 @@
     pass_on(a2, 2)
     share_far(3).start()
     share_far(4).start()
-
-    def first_multiplies(slot):
-        near_multiply(slot)
-        far_multiply(slot)
-
-    both(0, 3, first_multiplies)
     both(3, 7, near_in)
+    both(2, 5, near_multiply)
+    both(3, 5, far_multiply)
     pass_on(a2, 3)
     share_far(5).start()
     share_far(6).start()
-    both(3, 7, near_multiply)
     near_in(7)
+    both(5, 7, near_multiply)
 
     logit_copy.wait()
     raised = jnp.exp(lg[...] + lg_other[...])
@@ -304,9 +304,6 @@
 
     hn[0] = jax.nn.gelu(acc_n[...], approximate=True).astype(BF16)
     share_hidden(hn, 0).start()
-    pass_on(a2, 4)
-    share_far(7).start()
-    both(3, 7, far_multiply)
     for slot in range(Z):
         w2_copy(slot).wait()
         w2_share(slot).wait_recv()
@@ -337,12 +334,16 @@
         for p in NEAR_ORDER:
             bn(slot, p).start()
 
+    both(5, 7, far_multiply)
     share_hidden(hn, 0).wait_recv()
-    both(0, 4, near_out)
+    both(0, 1, near_out)
+    pass_on(a2, 4)
+    share_far(7).start()
+    both(1, 3, near_out)
     both(7, 8, far_multiply)
     hf[0] = jax.nn.gelu(acc_f[...], approximate=True).astype(BF16)
     share_hidden(hf, 1).start()
-    both(4, 8, near_out)
+    both(3, 5, near_out)
     share_hidden(hf, 1).wait_recv()
 
     def far_out(index):
@@ -383,16 +384,18 @@
     both(1, 3, far_out)
     both(0, 1, mix_down)
     reduce_step(bm, pm, rm, M_HALF, 1)
-    both(3, 8, far_out)
+    both(5, 7, near_out)
     reduce_step(bf, pf, rf, F_HALF, 2)
+    both(3, 5, far_out)
+    both(7, 8, near_out)
     both(1, 3, mix_down)
     reduce_step(bm, pm, rm, M_HALF, 2)
+    reduce_step(bf, pf, rf, F_HALF, 3)
+    both(5, 8, far_out)
     both(3, 5, mix_down)
-    reduce_step(bf, pf, rf, F_HALF, 3)
+    reduce_step(bf, pf, rf, F_HALF, 4)
     reduce_step(bm, pm, rm, M_HALF, 3)
     both(5, 8, mix_down)
-    reduce_step(bf, pf, rf, F_HALF, 4)
-    reduce_step(bm, pm, rm, M_HALF, 4)
 
     for way, half in back_parts_of(4):
         bf(4, way, half).wait_recv()
@@ -406,11 +409,12 @@
 
     for p in FAR_ORDER:
         far_back(p).start()
+    reduce_step(bm, pm, rm, M_HALF, 4)
+    remote(fr, ra, ra_send, ra_recv, sibling).wait_recv()
+    far_term[...] = jnp.dot(cf[...], ra[...], preferred_element_type=F32) + pm[0].astype(F32)
     for way, half in back_parts_of(4):
         bm(4, way, half).wait_recv()
-    partial = pm[0].astype(F32) + rm[0, 3].astype(F32) + rm[1, 3].astype(F32)
-    remote(fr, ra, ra_send, ra_recv, sibling).wait_recv()
-    out[...] = (partial + jnp.dot(cf[...], ra[...], preferred_element_type=F32)).astype(BF16)
+    out[...] = (far_term[...] + rm[0, 3].astype(F32) + rm[1, 3].astype(F32)).astype(BF16)
 
     for step in range(1, 5):
         for way, half in parts_of(step):
@@ -470,6 +474,7 @@
             pltpu.VMEM((EXPERTS, GROUP), F32),
             pltpu.VMEM((EXPERTS, GROUP), F32),
             pltpu.VMEM((8, GROUP), F32),
+            pltpu.VMEM((GROUP, W), F32),
             dma, dma((Z, 2)), dma((Z,)), dma((Z,)), dma((Z,)),
             dma((4, 2, 2)), dma((4, 2, 2)), dma, dma, dma((Z,)), dma((Z,)), dma((4, 2, 2)), dma((4, 2, 2)),
             dma((Z,)), dma((Z,)), dma((Z,)), dma((Z,)), dma((2,)), dma((2,)), dma, dma,

time: 79.5 us -> 71.8 us (0.903)
  the two profiles are of different devices: /device:TPU:8 before, /device:TPU:4 now
where the time goes in v2:
time: 71.8 us; the launch traced here: 71.6 us
  Pallas kernels  70 us (97%)
  local copies, waits for them, and re-layouts  1.57 us (2%)
    pallas_call x1, Pallas kernels, layer(): pl.pallas_call(kernel, out_shape=jax.ShapeDtypeStruct((GROUP, W), BF16),...  70 us
    unnamed x1, local copies, waits for them, and re-layouts  1.57 us

profile of v2, /device:TPU:4, one launch (start us, length us, event | category | flops | bytes accessed | tf_op | source)
XLA Modules:
  0.0 71.6 jit_solution(4817963638839569625)
XLA Ops:
  0.0 70.0 %experts.1 = bf16[256,256]{1,0:T(8,128)(2,1)} custom-call(bf16[256,256]{1,0:T(8,128)(2,1)} %tokens.1, s32[2,256]{1,0:T(2,128)} %bitcast.3, bf16[16,256]{1,0:T(8,128)(2,1)} %bitcast.2, bf16[1,4096,512]{2,1,0:T(8,128)(2,1)} %w_in.1, bf16[1,512,4096]{2,1,0:T(8,128)(2,1)} %w_out.1), custom_call_target="tpu_custom_call" | custom-call | tf_op jit(solution)/shard_map/experts/pallas_call | solution.py:446
  70.0 1.6 %copy.7 = bf16[256,256]{1,0:T(8,128)(2,1)} copy(bf16[256,256]{1,0:T(8,128)(2,1)} %experts.1) | data formatting | bytes 262144

commit v3 on v2

--- a/solution.py
+++ b/solution.py
@@ -30,7 +30,7 @@
 
 
 def back_parts_of(step):
-    return ((0, 0), (1, 1)) if step == 1 else ((0, 0), (1, 1), (0, 1), (1, 0))
+    return ((0, 0), (1, 1)) if step == 1 else ((0, 1), (1, 0), (0, 0), (1, 1))
 
 
 def offset_of(slot):
@@ -88,7 +88,7 @@
     def w1_copy(slot, side):
         rows = (ring(offset_of(slot)) * 2 + (core if side == 0 else 1 - core)) * W
         return pltpu.make_async_copy(
-            w_in.at[0, pl.ds(pl.multiple_of(rows, W), W), :], w1.at[slot, side], w1_sem.at[slot, side]
+            w_in.at[0, pl.ds(pl.multiple_of(rows, W), W), :], w1.at[pl.ds((slot * 2 + side) * W, W)], w1_sem
         )
 
     def w2_columns(slot, side):
@@ -96,11 +96,11 @@
         return w_out.at[0, :, pl.ds(pl.multiple_of(columns, W), W)]
 
     def w2_copy(slot):
-        return pltpu.make_async_copy(w2_columns(slot, 0), w2.at[slot, pl.ds(0, HID)], w2_sem.at[slot])
+        return pltpu.make_async_copy(w2_columns(slot, 0), w2.at[slot, pl.ds(0, HID)], w2_sem)
 
     def w2_share(slot):
         return remote(
-            w2_columns(slot, 1), w2.at[slot, pl.ds(HID, HID)], w2s_send.at[slot], w2s_recv.at[slot], sibling
+            w2_columns(slot, 1), w2.at[slot, pl.ds(HID, HID)], w2s_send, w2s_recv, sibling
         )
 
     def f1(step, way, half):
@@ -108,7 +108,7 @@
         start, size = T_HALF[half]
         return remote(
             tg.at[source, pl.ds(start, size)], tg.at[target, pl.ds(start, size)],
-            f1_send.at[step - 1, way, half], f1_recv.at[step - 1, way, half], along[way],
+            f1_send, f1_recv.at[step - 1, way, half], along[way],
         )
 
     def a1(p):
@@ -118,13 +118,13 @@
     def f2(slot, p):
         block = pl.ds(p * CAP, CAP)
         return remote(
-            near_send.at[slot, block], xn.at[slot, 0, block], f2_send.at[slot], f2_recv.at[slot], to[p]
+            near_send.at[slot, block], xn.at[slot, 0, block], f2_send, f2_recv.at[slot], to[p]
         )
 
     def f2_all(slot):
         block = pl.ds(0, NR - CAP)
         return remote(
-            near_send.at[slot, block], xn.at[slot, 0, block], f2_send.at[slot], f2_recv.at[slot], sibling
+            near_send.at[slot, block], xn.at[slot, 0, block], f2_send, f2_recv.at[slot], sibling
         )
 
     def a2(step, way, half):
@@ -132,14 +132,14 @@
         start, size = F_HALF[half]
         return remote(
             xf.at[source, 0, pl.ds(start, size)], xf.at[target, 0, pl.ds(start, size)],
-            a2_send.at[step - 1, way, half], a2_recv.at[step - 1, way, half], along[way],
+            a2_send, a2_recv.at[step - 1, way, half], along[way],
         )
 
     def share_near(slot):
-        return remote(xn.at[slot, 0], xn.at[slot, 1], sn_send.at[slot], sn_recv.at[slot], sibling)
+        return remote(xn.at[slot, 0], xn.at[slot, 1], sn_send, sn_recv.at[slot], sibling)
 
     def share_far(slot):
-        return remote(xf.at[slot, 0], xf.at[slot, 1], sf_send.at[slot], sf_recv.at[slot], sibling)
+        return remote(xf.at[slot, 0], xf.at[slot, 1], sf_send, sf_recv.at[slot], sibling)
 
     def send_near(slot):
         for p in NEAR_ORDER:
@@ -212,28 +212,39 @@
         dispatch_near(slot)
         send_near(slot)
 
-    def multiply(rows_of, total, side):
-        def work(slot):
-            total[...] += jnp.dot(rows_of[slot, side], w1[slot, side], preferred_element_type=F32)
-
-        return work
+    def multiply(rows_of, total, slot, count):
+        columns = [rows_of[slot + i, side] for i in range(count) for side in range(2)]
+        depth = 2 * W * count
+        start = pl.multiple_of(slot * 2 * W, 2 * W)
+        total[...] += jnp.dot(
+            jnp.concatenate(columns, axis=1), w1[pl.ds(start, depth), :], preferred_element_type=F32
+        )
 
     def near_in(slot):
         f2_all(slot).wait_recv()
         share_near(slot).start()
 
-    def near_multiply(slot):
-        multiply(xn, acc_n, 0)(slot)
-        share_near(slot).wait_recv()
-        multiply(xn, acc_n, 1)(slot)
-
-    def far_multiply(slot):
-        multiply(xf, acc_f, 0)(slot)
-        share_far(slot).wait_recv()
-        multiply(xf, acc_f, 1)(slot)
+    def near_multiply(slot, count=1):
+        for i in range(count):
+            share_near(slot + i).wait_recv()
+        multiply(xn, acc_n, slot, count)
+
+    def far_multiply(slot, count=1):
+        for i in range(count):
+            share_far(slot + i).wait_recv()
+        multiply(xf, acc_f, slot, count)
+
+    def w2_shares(lower, upper):
+        for slot in range(lower, upper):
+            w2_share(slot).start()
+
+    def w2_shares(lower, upper):
+        for slot in range(lower, upper):
+            w2_share(slot).start()
 
     pass_on(f1, 1)
     both(1, 3, near_part)
+    w2_shares(0, 2)
     pl_all = pl.ds(0, FR)
     remote(far_send.at[pl_all], xf.at[0, 0, pl_all], a1_send, a1_recv, sibling).wait_recv()
     for way, half in parts_of(1):
@@ -242,38 +253,126 @@
     pass_on(f1, 2)
     both(3, 5, near_part)
     near_in(0)
-    for slot in range(Z):
-        for side in range(2):
-            w1_copy(slot, side).wait()
-    both(0, 1, far_multiply)
+    w2_shares(2, 4)
+    pltpu.make_async_copy(w_in.at[0], w1, w1_sem).wait()
     pass_on(a2, 1)
     share_far(1).start()
     share_far(2).start()
-    both(0, 1, near_multiply)
     pass_on(f1, 3)
     both(5, 7, near_part)
     both(1, 3, near_in)
-    for slot in range(Z):
-        w2_share(slot).start()
-    both(1, 3, far_multiply)
-    both(1, 2, near_multiply)
-    pass_on(f1, 4)
-    both(7, 8, near_part)
-
-    logit_copy = remote(lg, lg_other, l_send, l_recv, sibling)
-    logit_copy.start()
+    w2_shares(4, 6)
+    far_multiply(0, 1)
+    near_multiply(0, 1)
     pass_on(a2, 2)
     share_far(3).start()
     share_far(4).start()
-    both(3, 7, near_in)
-    both(2, 5, near_multiply)
-    both(3, 5, far_multiply)
+    pass_on(f1, 4)
+    both(7, 8, near_part)
+    w2_shares(6, 8)
+
+    logit_copy = remote(lg, lg_other, l_send, l_recv, sibling)
+    logit_copy.start()
+    both(3, 5, near_in)
+    far_multiply(1, 2)
     pass_on(a2, 3)
     share_far(5).start()
     share_far(6).start()
+    near_multiply(1, 2)
+    both(5, 7, near_in)
+    far_multiply(3, 2)
+    near_multiply(3, 2)
+    pass_on(a2, 4)
+    share_far(7).start()
     near_in(7)
-    both(5, 7, near_multiply)
-
+    near_multiply(5, 2)
+    near_multiply(7, 1)
+
+    def share_hidden(buffer, which):
+        return remote(
+            buffer.at[0], buffer.at[1], h_send.at[which], h_recv.at[which], sibling
+        )
+
+    hn[0] = jax.nn.gelu(acc_n[...], approximate=True).astype(BF16)
+    share_hidden(hn, 0).start()
+    far_multiply(5, 2)
+    far_multiply(7, 1)
+    hf[0] = jax.nn.gelu(acc_f[...], approximate=True).astype(BF16)
+    share_hidden(hf, 1).start()
+    own_half, other_half = w2.at[:, pl.ds(0, HID)], w2.at[:, pl.ds(HID, HID)]
+    pltpu.make_async_copy(own_half, own_half, w2_sem).wait()
+    w2_all = remote(own_half, other_half, w2s_send, w2s_recv, sibling)
+    w2_all.wait_recv()
+
+    def bn(slot, p):
+        block = pl.ds(p * CAP, CAP)
+        return remote(
+            pn.at[slot, block], rn.at[slot, block], bn_send, bn_recv.at[slot], back[p]
+        )
+
+    def bn_all(slot):
+        block = pl.ds(0, NR - CAP)
+        return remote(
+            pn.at[slot, block], rn.at[slot, block], bn_send, bn_recv.at[slot], sibling
+        )
+
+    def second(buffer, slot):
+        return jnp.dot(
+            jnp.concatenate([buffer[0], buffer[1]], axis=1), w2[slot], preferred_element_type=F32
+        ).astype(BF16)
+
+    def near_out(index):
+        slot = 7 - index
+        terms = second(hn, slot)
+        pn[slot] = terms
+        rn[slot, SELF * CAP:(SELF + 1) * CAP, :] = terms[SELF * CAP:(SELF + 1) * CAP, :]
+        for p in NEAR_ORDER:
+            bn(slot, p).start()
+
+    def far_out(index):
+        slot = 7 - index
+        pf[slot] = second(hf, slot)
+
+    def reduce_copy(own, received, halves, send, recv, step, way, half):
+        start, size = halves[half]
+        return remote(
+            own.at[back_slot(step, way), pl.ds(start, size)], received.at[way, step - 1, pl.ds(start, size)],
+            send, recv.at[step - 1, way, half], along[way],
+        )
+
+    bf = functools.partial(reduce_copy, pf, rf, F_HALF, bf_send, bf_recv)
+    bm = functools.partial(reduce_copy, pm, rm, M_HALF, bm_send, bm_recv)
+
+    def reduce_step(transfer, own, received, halves, step, chosen=None):
+        for way, half in chosen or back_parts_of(step):
+            if step > 1 and (way, half) in back_parts_of(step - 1):
+                transfer(step - 1, way, half).wait_recv()
+                start, size = halves[half]
+                slot = back_slot(step, way)
+                own[slot, start:start + size, :] = (
+                    own[slot, start:start + size, :].astype(F32)
+                    + received[way, step - 2, start:start + size, :].astype(F32)
+                ).astype(BF16)
+            transfer(step, way, half).start()
+
+    fresh, held = ((0, 1), (1, 0)), ((0, 0), (1, 1))
+
+    def mix(slot):
+        bn_all(slot).wait_recv()
+        pm[slot] = jnp.dot(cn[...], rn[slot], preferred_element_type=F32).astype(BF16)
+
+    def mix_down(index):
+        mix(7 - index)
+
+    share_hidden(hn, 0).wait_recv()
+    both(0, 1, near_out)
+    share_hidden(hf, 1).wait_recv()
+    both(0, 1, far_out)
+    reduce_step(bf, pf, rf, F_HALF, 1)
+    both(1, 2, near_out)
+    both(1, 3, far_out)
+    reduce_step(bf, pf, rf, F_HALF, 2, fresh)
+    both(2, 3, near_out)
     logit_copy.wait()
     raised = jnp.exp(lg[...] + lg_other[...])
     probs = raised / jnp.sum(raised, axis=0, keepdims=True)
@@ -295,107 +394,28 @@
     cn[...] = weights(0, NR)
     cf[...] = weights(NR, FR)
 
-    both(7, 8, near_multiply)
-
-    def share_hidden(buffer, which):
-        return remote(
-            buffer.at[0], buffer.at[1], h_send.at[which], h_recv.at[which], sibling
-        )
-
-    hn[0] = jax.nn.gelu(acc_n[...], approximate=True).astype(BF16)
-    share_hidden(hn, 0).start()
-    for slot in range(Z):
-        w2_copy(slot).wait()
-        w2_share(slot).wait_recv()
-
-    def bn(slot, p):
-        block = pl.ds(p * CAP, CAP)
-        return remote(
-            pn.at[slot, block], rn.at[slot, block], bn_send.at[slot], bn_recv.at[slot], back[p]
-        )
-
-    def bn_all(slot):
-        block = pl.ds(0, NR - CAP)
-        return remote(
-            pn.at[slot, block], rn.at[slot, block], bn_send.at[slot], bn_recv.at[slot], sibling
-        )
-
-    def second(buffer, slot):
-        return (
-            jnp.dot(buffer[0], w2[slot, 0:HID, :], preferred_element_type=F32)
-            + jnp.dot(buffer[1], w2[slot, HID:2 * HID, :], preferred_element_type=F32)
-        ).astype(BF16)
-
-    def near_out(index):
-        slot = 7 - index
-        terms = second(hn, slot)
-        pn[slot] = terms
-        rn[slot, SELF * CAP:(SELF + 1) * CAP, :] = terms[SELF * CAP:(SELF + 1) * CAP, :]
-        for p in NEAR_ORDER:
-            bn(slot, p).start()
-
-    both(5, 7, far_multiply)
-    share_hidden(hn, 0).wait_recv()
-    both(0, 1, near_out)
-    pass_on(a2, 4)
-    share_far(7).start()
-    both(1, 3, near_out)
-    both(7, 8, far_multiply)
-    hf[0] = jax.nn.gelu(acc_f[...], approximate=True).astype(BF16)
-    share_hidden(hf, 1).start()
-    both(3, 5, near_out)
-    share_hidden(hf, 1).wait_recv()
-
-    def far_out(index):
-        slot = 7 - index
-        pf[slot] = second(hf, slot)
-
-    def reduce_copy(own, received, halves, send, recv, step, way, half):
-        start, size = halves[half]
-        return remote(
-            own.at[back_slot(step, way), pl.ds(start, size)], received.at[way, step - 1, pl.ds(start, size)],
-            send.at[step - 1, way, half], recv.at[step - 1, way, half], along[way],
-        )
-
-    bf = functools.partial(reduce_copy, pf, rf, F_HALF, bf_send, bf_recv)
-    bm = functools.partial(reduce_copy, pm, rm, M_HALF, bm_send, bm_recv)
-
-    def reduce_step(transfer, own, received, halves, step):
-        for way, half in back_parts_of(step):
-            if step > 1 and (way, half) in back_parts_of(step - 1):
-                transfer(step - 1, way, half).wait_recv()
-                start, size = halves[half]
-                slot = back_slot(step, way)
-                own[slot, start:start + size, :] = (
-                    own[slot, start:start + size, :].astype(F32)
-                    + received[way, step - 2, start:start + size, :].astype(F32)
-                ).astype(BF16)
-            transfer(step, way, half).start()
-
-    def mix(slot):
-        bn_all(slot).wait_recv()
-        pm[slot] = jnp.dot(cn[...], rn[slot], preferred_element_type=F32).astype(BF16)
-
-    def mix_down(index):
-        mix(7 - index)
-
-    both(0, 1, far_out)
-    reduce_step(bf, pf, rf, F_HALF, 1)
-    both(1, 3, far_out)
+    both(3, 4, near_out)
+    both(3, 5, far_out)
+    reduce_step(bf, pf, rf, F_HALF, 2, held)
+    both(4, 5, near_out)
+    reduce_step(bf, pf, rf, F_HALF, 3, fresh)
+    both(5, 7, far_out)
+    both(5, 6, near_out)
     both(0, 1, mix_down)
     reduce_step(bm, pm, rm, M_HALF, 1)
-    both(5, 7, near_out)
-    reduce_step(bf, pf, rf, F_HALF, 2)
-    both(3, 5, far_out)
+    both(6, 7, near_out)
+    reduce_step(bf, pf, rf, F_HALF, 3, held)
+    reduce_step(bf, pf, rf, F_HALF, 4, fresh)
+    both(1, 2, mix_down)
+    reduce_step(bm, pm, rm, M_HALF, 2, fresh[:1])
     both(7, 8, near_out)
-    both(1, 3, mix_down)
-    reduce_step(bm, pm, rm, M_HALF, 2)
-    reduce_step(bf, pf, rf, F_HALF, 3)
-    both(5, 8, far_out)
+    both(2, 3, mix_down)
+    reduce_step(bm, pm, rm, M_HALF, 2, fresh[1:])
+    both(7, 8, far_out)
+    reduce_step(bm, pm, rm, M_HALF, 2, held)
+    reduce_step(bf, pf, rf, F_HALF, 4, held)
     both(3, 5, mix_down)
-    reduce_step(bf, pf, rf, F_HALF, 4)
     reduce_step(bm, pm, rm, M_HALF, 3)
-    both(5, 8, mix_down)
 
     for way, half in back_parts_of(4):
         bf(4, way, half).wait_recv()
@@ -409,32 +429,30 @@
 
     for p in FAR_ORDER:
         far_back(p).start()
+    both(5, 7, mix_down)
     reduce_step(bm, pm, rm, M_HALF, 4)
+    both(7, 8, mix_down)
     remote(fr, ra, ra_send, ra_recv, sibling).wait_recv()
     far_term[...] = jnp.dot(cf[...], ra[...], preferred_element_type=F32) + pm[0].astype(F32)
     for way, half in back_parts_of(4):
         bm(4, way, half).wait_recv()
     out[...] = (far_term[...] + rm[0, 3].astype(F32) + rm[1, 3].astype(F32)).astype(BF16)
 
-    for step in range(1, 5):
-        for way, half in parts_of(step):
-            f1(step, way, half).wait_send()
-            a2(step, way, half).wait_send()
-        for way, half in back_parts_of(step):
-            bf(step, way, half).wait_send()
-            bm(step, way, half).wait_send()
-    remote(far_send.at[pl_all], xf.at[0, 0, pl_all], a1_send, a1_recv, sibling).wait_send()
-    remote(fr, ra, ra_send, ra_recv, sibling).wait_send()
-
-    def sent(slot):
-        f2_all(slot).wait_send()
-        bn_all(slot).wait_send()
-        share_near(slot).wait_send()
-        share_far(slot).wait_send()
-
-    both(0, Z, sent)
-    for slot in range(Z):
-        w2_share(slot).wait_send()
+    def sent(ref, semaphore):
+        remote(ref, ref, semaphore, semaphore, sibling).wait_send()
+
+    ring_blocks, most = pl.ds(0, Z - 1), pl.ds(0, NR - CAP)
+    sent(tg.at[ring_blocks], f1_send)
+    sent(far_send, a1_send)
+    sent(near_send.at[:, most], f2_send)
+    sent(xf.at[ring_blocks, 0], a2_send)
+    sent(xn.at[:, 0], sn_send)
+    sent(xf.at[:, 0], sf_send)
+    sent(pf.at[ring_blocks], bf_send)
+    sent(pm.at[ring_blocks], bm_send)
+    sent(pn.at[:, most], bn_send)
+    sent(fr, ra_send)
+    w2_all.wait_send()
     share_hidden(hn, 0).wait_send()
     share_hidden(hf, 1).wait_send()
 
@@ -457,7 +475,7 @@
             pltpu.VMEM((Z, 2, FR, W), BF16),
             pltpu.VMEM((NR, HID), F32),
             pltpu.VMEM((FR, HID), F32),
-            pltpu.VMEM((Z, 2, W, HID), BF16),
+            pltpu.VMEM((Z * 2 * W, HID), BF16),
             pltpu.VMEM((Z, 2 * HID, W), BF16),
             pltpu.VMEM((2, NR, HID), BF16),
             pltpu.VMEM((2, FR, HID), BF16),
@@ -475,10 +493,10 @@
             pltpu.VMEM((EXPERTS, GROUP), F32),
             pltpu.VMEM((8, GROUP), F32),
             pltpu.VMEM((GROUP, W), F32),
-            dma, dma((Z, 2)), dma((Z,)), dma((Z,)), dma((Z,)),
-            dma((4, 2, 2)), dma((4, 2, 2)), dma, dma, dma((Z,)), dma((Z,)), dma((4, 2, 2)), dma((4, 2, 2)),
-            dma((Z,)), dma((Z,)), dma((Z,)), dma((Z,)), dma((2,)), dma((2,)), dma, dma,
-            dma((4, 2, 2)), dma((4, 2, 2)), dma((Z,)), dma((Z,)), dma((4, 2, 2)), dma((4, 2, 2)), dma, dma,
+            dma, dma, dma, dma, dma,
+            dma, dma((4, 2, 2)), dma, dma, dma, dma((Z,)), dma, dma((4, 2, 2)),
+            dma, dma((Z,)), dma, dma((Z,)), dma((2,)), dma((2,)), dma, dma,
+            dma, dma((4, 2, 2)), dma, dma((Z,)), dma, dma((4, 2, 2)), dma, dma,
         ],
         compiler_params=pltpu.CompilerParams(collective_id=0, has_side_effects=True),
         name="experts",

time: 71.8 us -> 67.5 us (0.940)
  the two profiles are of different devices: /device:TPU:4 before, /device:TPU:1 now
where the time goes in v3:
time: 67.5 us; the launch traced here: 66.7 us
  Pallas kernels  65.2 us (97%)
  local copies, waits for them, and re-layouts  1.57 us (2%)
    pallas_call x1, Pallas kernels, layer(): pl.pallas_call(kernel, out_shape=jax.ShapeDtypeStruct((GROUP, W), BF16),...  65.2 us
    unnamed x1, local copies, waits for them, and re-layouts  1.57 us

profile of v3, /device:TPU:1, one launch (start us, length us, event | category | flops | bytes accessed | tf_op | source)
XLA Modules:
  0.0 66.7 jit_solution(7784292513744547214)
XLA Ops:
  0.0 65.2 %experts.1 = bf16[256,256]{1,0:T(8,128)(2,1)} custom-call(bf16[256,256]{1,0:T(8,128)(2,1)} %tokens.1, s32[2,256]{1,0:T(2,128)} %bitcast.3, bf16[16,256]{1,0:T(8,128)(2,1)} %bitcast.2, bf16[1,4096,512]{2,1,0:T(8,128)(2,1)} %w_in.1, bf16[1,512,4096]{2,1,0:T(8,128)(2,1)} %w_out.1), custom_call_target="tpu_custom_call" | custom-call | tf_op jit(solution)/shard_map/experts/pallas_call | solution.py:464
  65.2 1.6 %copy.7 = bf16[256,256]{1,0:T(8,128)(2,1)} copy(bf16[256,256]{1,0:T(8,128)(2,1)} %experts.1) | data formatting | bytes 262144

commit v4 on v3

--- a/solution.py
+++ b/solution.py
@@ -47,10 +47,10 @@
 
 
 def kernel(
-    tokens, routing, gate, w_in, w_out, out,
+    tokens, picks, gate, w_in, w_out, out,
     tg, assign, near_send, far_send, xn, xf, acc_n, acc_f, w1, w2, hn, hf,
-    pf, rf, pn, rn, pm, rm, fr, ra, cn, cf, lg, lg_other, base, far_term,
-    tok_sem, w1_sem, w2_sem, w2s_send, w2s_recv,
+    pf, rf, pn, rn, pm, rm, fr, ra, cn, cf, lg, lg_other, base, far_term, routing,
+    tok_sem, gate_sem, picks_sem, w1_sem, w2_sem, w2s_send, w2s_recv,
     f1_send, f1_recv, a1_send, a1_recv, f2_send, f2_recv, a2_send, a2_recv,
     sn_send, sn_recv, sf_send, sf_recv, h_send, h_recv, l_send, l_recv,
     bf_send, bf_recv, bn_send, bn_recv, bm_send, bm_recv, ra_send, ra_recv,
@@ -68,7 +68,7 @@
 
     to = [plane(dx, dy) for dx, dy in SHIFTS]
     back = [plane(-dx, -dy) for dx, dy in SHIFTS]
-    along = ((dp, ring(1) * 2 + core), (dp, ring(-1) * 2 + core))
+    along = ((dp, ring(1) * 2 + 1 - core), (dp, ring(-1) * 2 + 1 - core))
     sibling = (dp, z * 2 + 1 - core)
 
     def remote(src, dst, send, recv, device):
@@ -81,18 +81,26 @@
     for device in [to[p] for p in range(EXPERTS) if p != SELF] + [*along, sibling]:
         pl.semaphore_signal(barrier, inc=1, device_id=device, device_id_type=MESH)
 
+    picks_copy = pltpu.make_async_copy(picks, routing, picks_sem)
+    picks_copy.start()
     token_copy = pltpu.make_async_copy(tokens, tg.at[0, pl.ds(0, GROUP)], tok_sem)
     token_copy.start()
-    tg[0, GROUP:TB, :] = gate[...]
+    gate_copy = pltpu.make_async_copy(gate, tg.at[0, pl.ds(GROUP, EXPERTS)], gate_sem)
+    gate_copy.start()
+    picks_copy.wait()
+
+    def block_of(slot, side):
+        offset = offset_of(slot)
+        return ring(offset) * 2 + (core if (offset + side) % 2 == 0 else 1 - core)
 
     def w1_copy(slot, side):
-        rows = (ring(offset_of(slot)) * 2 + (core if side == 0 else 1 - core)) * W
+        rows = block_of(slot, side) * W
         return pltpu.make_async_copy(
             w_in.at[0, pl.ds(pl.multiple_of(rows, W), W), :], w1.at[pl.ds((slot * 2 + side) * W, W)], w1_sem
         )
 
     def w2_columns(slot, side):
-        columns = (ring(offset_of(slot)) * 2 + (core if side == 0 else 1 - core)) * W
+        columns = block_of(slot, side) * W
         return w_out.at[0, :, pl.ds(pl.multiple_of(columns, W), W)]
 
     def w2_copy(slot):
@@ -177,6 +185,7 @@
     lg[...] = jnp.zeros_like(lg)
 
     token_copy.wait()
+    gate_copy.wait()
     pl.semaphore_wait(barrier, 18)
     for way, half in parts_of(1):
         f1(1, way, half).start()
@@ -238,13 +247,12 @@
         for slot in range(lower, upper):
             w2_share(slot).start()
 
-    def w2_shares(lower, upper):
-        for slot in range(lower, upper):
-            w2_share(slot).start()
-
+    for slot in range(4):
+        w2_share(slot).start()
     pass_on(f1, 1)
     both(1, 3, near_part)
-    w2_shares(0, 2)
+    for slot in range(4, Z):
+        w2_share(slot).start()
     pl_all = pl.ds(0, FR)
     remote(far_send.at[pl_all], xf.at[0, 0, pl_all], a1_send, a1_recv, sibling).wait_recv()
     for way, half in parts_of(1):
@@ -253,7 +261,6 @@
     pass_on(f1, 2)
     both(3, 5, near_part)
     near_in(0)
-    w2_shares(2, 4)
     pltpu.make_async_copy(w_in.at[0], w1, w1_sem).wait()
     pass_on(a2, 1)
     share_far(1).start()
@@ -261,7 +268,6 @@
     pass_on(f1, 3)
     both(5, 7, near_part)
     both(1, 3, near_in)
-    w2_shares(4, 6)
     far_multiply(0, 1)
     near_multiply(0, 1)
     pass_on(a2, 2)
@@ -269,7 +275,6 @@
     share_far(4).start()
     pass_on(f1, 4)
     both(7, 8, near_part)
-    w2_shares(6, 8)
 
     logit_copy = remote(lg, lg_other, l_send, l_recv, sibling)
     logit_copy.start()
@@ -285,20 +290,20 @@
     pass_on(a2, 4)
     share_far(7).start()
     near_in(7)
+    far_multiply(5, 2)
     near_multiply(5, 2)
+    far_multiply(7, 1)
+
+    def share_hidden(buffer, which):
+        return remote(
+            buffer.at[:, pl.ds(0, HID)], buffer.at[:, pl.ds(HID, HID)], h_send.at[which], h_recv.at[which], sibling,
+        )
+
+    hf[:, 0:HID] = jax.nn.gelu(acc_f[...], approximate=True).astype(BF16)
+    share_hidden(hf, 1).start()
     near_multiply(7, 1)
-
-    def share_hidden(buffer, which):
-        return remote(
-            buffer.at[0], buffer.at[1], h_send.at[which], h_recv.at[which], sibling
-        )
-
-    hn[0] = jax.nn.gelu(acc_n[...], approximate=True).astype(BF16)
+    hn[:, 0:HID] = jax.nn.gelu(acc_n[...], approximate=True).astype(BF16)
     share_hidden(hn, 0).start()
-    far_multiply(5, 2)
-    far_multiply(7, 1)
-    hf[0] = jax.nn.gelu(acc_f[...], approximate=True).astype(BF16)
-    share_hidden(hf, 1).start()
     own_half, other_half = w2.at[:, pl.ds(0, HID)], w2.at[:, pl.ds(HID, HID)]
     pltpu.make_async_copy(own_half, own_half, w2_sem).wait()
     w2_all = remote(own_half, other_half, w2s_send, w2s_recv, sibling)
@@ -317,9 +322,7 @@
         )
 
     def second(buffer, slot):
-        return jnp.dot(
-            jnp.concatenate([buffer[0], buffer[1]], axis=1), w2[slot], preferred_element_type=F32
-        ).astype(BF16)
+        return jnp.dot(buffer[...], w2[slot], preferred_element_type=F32).astype(BF16)
 
     def near_out(index):
         slot = 7 - index
@@ -364,14 +367,13 @@
     def mix_down(index):
         mix(7 - index)
 
-    share_hidden(hn, 0).wait_recv()
-    both(0, 1, near_out)
     share_hidden(hf, 1).wait_recv()
     both(0, 1, far_out)
     reduce_step(bf, pf, rf, F_HALF, 1)
-    both(1, 2, near_out)
     both(1, 3, far_out)
     reduce_step(bf, pf, rf, F_HALF, 2, fresh)
+    share_hidden(hn, 0).wait_recv()
+    both(0, 2, near_out)
     both(2, 3, near_out)
     logit_copy.wait()
     raised = jnp.exp(lg[...] + lg_other[...])
@@ -464,7 +466,7 @@
     return pl.pallas_call(
         kernel,
         out_shape=jax.ShapeDtypeStruct((GROUP, W), BF16),
-        in_specs=[anywhere, vmem, vmem, anywhere, anywhere],
+        in_specs=[anywhere] * 5,
         out_specs=vmem,
         scratch_shapes=[
             pltpu.VMEM((Z, TB, W), BF16),
@@ -477,8 +479,8 @@
             pltpu.VMEM((FR, HID), F32),
             pltpu.VMEM((Z * 2 * W, HID), BF16),
             pltpu.VMEM((Z, 2 * HID, W), BF16),
-            pltpu.VMEM((2, NR, HID), BF16),
-            pltpu.VMEM((2, FR, HID), BF16),
+            pltpu.VMEM((NR, 2 * HID), BF16),
+            pltpu.VMEM((FR, 2 * HID), BF16),
             pltpu.VMEM((Z, FR, W), BF16),
             pltpu.VMEM((2, 4, FR, W), BF16),
             pltpu.VMEM((Z, NR, W), BF16),
@@ -493,7 +495,8 @@
             pltpu.VMEM((EXPERTS, GROUP), F32),
             pltpu.VMEM((8, GROUP), F32),
             pltpu.VMEM((GROUP, W), F32),
-            dma, dma, dma, dma, dma,
+            pltpu.VMEM((2, GROUP), jnp.int32),
+            dma, dma, dma, dma, dma, dma, dma,
             dma, dma((4, 2, 2)), dma, dma, dma, dma((Z,)), dma, dma((4, 2, 2)),
             dma, dma((Z,)), dma, dma((Z,)), dma((2,)), dma((2,)), dma, dma,
             dma, dma((4, 2, 2)), dma, dma((Z,)), dma, dma((4, 2, 2)), dma, dma,

time: 67.5 us -> 65.6 us (0.972); the launches traced: 66.7 us -> 65.5 us
  Pallas kernels: 65.2 us -> 63.9 us
    pallas_call x1, Pallas kernels: 65.2 us -> 63.9 us  [layer(): pl.pallas_call(kernel, out_shape=jax.ShapeDtypeStruct((GROUP, W), BF16),...]
where the time goes in v4:
time: 65.6 us; the launch traced here: 65.5 us
  Pallas kernels  63.9 us (97%)
  local copies, waits for them, and re-layouts  1.57 us (2%)
    pallas_call x1, Pallas kernels, layer(): pl.pallas_call(kernel, out_shape=jax.ShapeDtypeStruct((GROUP, W), BF16),...  63.9 us
    unnamed x1, local copies, waits for them, and re-layouts  1.57 us

profile of v4, /device:TPU:1, one launch (start us, length us, event | category | flops | bytes accessed | tf_op | source)
XLA Modules:
  0.0 65.5 jit_solution(18320930835661453714)
XLA Ops:
  0.0 63.9 %experts.1 = bf16[256,256]{1,0:T(8,128)(2,1)} custom-call(bf16[256,256]{1,0:T(8,128)(2,1)} %tokens.1, s32[2,256]{1,0:T(2,128)} %bitcast.3, bf16[16,256]{1,0:T(8,128)(2,1)} %bitcast.2, bf16[1,4096,512]{2,1,0:T(8,128)(2,1)} %w_in.1, bf16[1,512,4096]{2,1,0:T(8,128)(2,1)} %w_out.1), custom_call_target="tpu_custom_call" | custom-call | tf_op jit(solution)/shard_map/experts/pallas_call | solution.py:466
  63.9 1.6 %copy.7 = bf16[256,256]{1,0:T(8,128)(2,1)} copy(bf16[256,256]{1,0:T(8,128)(2,1)} %experts.1) | data formatting | bytes 262144

commit v5 on v4

--- a/solution.py
+++ b/solution.py
@@ -465,7 +465,7 @@
     dma = pltpu.SemaphoreType.DMA
     return pl.pallas_call(
         kernel,
-        out_shape=jax.ShapeDtypeStruct((GROUP, W), BF16),
+        out_shape=pltpu.VMEM((GROUP, W), BF16),
         in_specs=[anywhere] * 5,
         out_specs=vmem,
         scratch_shapes=[

time: 65.6 us -> 64 us (0.976)
  local copies, waits for them, and re-layouts: 1.57 us -> 0.66 us
    unnamed x1, local copies, waits for them, and re-layouts: 1.57 us -> 0.66 us
where the time goes in v5:
time: 64 us
  Pallas kernels  63.3 us (99%)
  local copies, waits for them, and re-layouts  0.66 us (1%)
    pallas_call x1, Pallas kernels, layer(): pl.pallas_call(kernel, out_shape=pltpu.VMEM((GROUP, W), BF16), in_specs=[...  63.3 us

profile of v5, /device:TPU:1, one launch (start us, length us, event | category | flops | bytes accessed | tf_op | source)
XLA Modules:
  0.0 64.0 jit_solution(8554409649792256966)
XLA Ops:
  0.0 63.3 %experts.1 = bf16[256,256]{1,0:T(8,128)(2,1)S(1)} custom-call(bf16[256,256]{1,0:T(8,128)(2,1)} %tokens.1, s32[2,256]{1,0:T(2,128)} %bitcast.3, bf16[16,256]{1,0:T(8,128)(2,1)} %bitcast.2, bf16[1,4096,512]{2,1,0:T(8,128)(2,1)} %w_in.1, bf16[1,512,4096]{2,1,0:T(8,128)(2,1)} %w_out.1), custom_call_target="tpu_custom_call" | custom-call | tf_op jit(solution)/shard_map/experts/pallas_call | solution.py:466
  63.3 0.7 %copy.7 = bf16[256,256]{1,0:T(8,128)(2,1)} copy(bf16[256,256]{1,0:T(8,128)(2,1)S(1)} %experts.1) | data formatting | bytes 262144

commit v6 on v5

--- a/solution.py
+++ b/solution.py
@@ -20,17 +20,28 @@
 NEAR_ORDER = [1, 3, 7, 5, 9, 10, 0, 8, 2, 6]
 FAR_ORDER = [13, 11, 14, 12, 15]
 TB = GROUP + EXPERTS
-T_HALF = ((0, 128), (128, TB - 128))
-F_HALF = ((0, 3 * CAP), (3 * CAP, FR - 3 * CAP))
-M_HALF = ((0, 128), (128, 128))
-
-
-def parts_of(step):
-    return ((0, 0), (1, 1)) if step == 4 else ((0, 0), (1, 1), (0, 1), (1, 0))
-
-
-def back_parts_of(step):
-    return ((0, 0), (1, 1)) if step == 1 else ((0, 1), (1, 0), (0, 0), (1, 1))
+T_PIECES = ((0, 128), (128, TB - 128))
+F_PIECES = ((0, 3 * CAP), (3 * CAP, FR - 3 * CAP))
+M_PIECES = ((0, 128), (128, 128))
+N_PIECES = ((0, 6 * CAP), (6 * CAP, NR - 6 * CAP))
+
+
+def far_parts(count):
+    half = count // 2
+    return [(way, i + half * way) for i in range(half) for way in (0, 1)]
+
+
+def short_parts(count):
+    half = count // 2
+    return [(way, i + half * (1 - way)) for i in range(half) for way in (0, 1)]
+
+
+def parts_of(step, count):
+    return far_parts(count) if step == 4 else far_parts(count) + short_parts(count)
+
+
+def back_parts_of(step, count):
+    return far_parts(count) if step == 1 else short_parts(count) + far_parts(count)
 
 
 def offset_of(slot):
@@ -113,7 +124,7 @@
 
     def f1(step, way, half):
         source, target = gather_slots(step, way)
-        start, size = T_HALF[half]
+        start, size = T_PIECES[half]
         return remote(
             tg.at[source, pl.ds(start, size)], tg.at[target, pl.ds(start, size)],
             f1_send, f1_recv.at[step - 1, way, half], along[way],
@@ -137,7 +148,7 @@
 
     def a2(step, way, half):
         source, target = gather_slots(step, way)
-        start, size = F_HALF[half]
+        start, size = F_PIECES[half]
         return remote(
             xf.at[source, 0, pl.ds(start, size)], xf.at[target, 0, pl.ds(start, size)],
             a2_send, a2_recv.at[step - 1, way, half], along[way],
@@ -153,10 +164,10 @@
         for p in NEAR_ORDER:
             f2(slot, p).start()
 
-    def pass_on(transfer, step):
-        for way, half in parts_of(step):
+    def pass_on(transfer, step, chosen=None):
+        for way, half in chosen or parts_of(step, 2):
             transfer(step, way, half).wait_recv()
-            if step < 4 and (way, half) in parts_of(step + 1):
+            if step < 4 and (way, half) in parts_of(step + 1, 2):
                 transfer(step + 1, way, half).start()
 
     names = lax.broadcasted_iota(jnp.int32, (EXPERTS, GROUP), 0)
@@ -187,7 +198,7 @@
     token_copy.wait()
     gate_copy.wait()
     pl.semaphore_wait(barrier, 18)
-    for way, half in parts_of(1):
+    for way, half in parts_of(1, 2):
         f1(1, way, half).start()
     far_send[...] = jnp.dot(
         assign[NR:, :], tg[0, 0:GROUP, :], preferred_element_type=F32
@@ -255,55 +266,70 @@
         w2_share(slot).start()
     pl_all = pl.ds(0, FR)
     remote(far_send.at[pl_all], xf.at[0, 0, pl_all], a1_send, a1_recv, sibling).wait_recv()
-    for way, half in parts_of(1):
+    for way, half in far_parts(2):
         a2(1, way, half).start()
     share_far(0).start()
     pass_on(f1, 2)
+    for way, half in short_parts(2):
+        a2(1, way, half).start()
     both(3, 5, near_part)
     near_in(0)
     pltpu.make_async_copy(w_in.at[0], w1, w1_sem).wait()
-    pass_on(a2, 1)
-    share_far(1).start()
-    share_far(2).start()
+    pass_on(a2, 1, far_parts(2))
+    near_multiply(0, 1)
+    far_multiply(0, 1)
     pass_on(f1, 3)
     both(5, 7, near_part)
     both(1, 3, near_in)
-    far_multiply(0, 1)
-    near_multiply(0, 1)
-    pass_on(a2, 2)
-    share_far(3).start()
-    share_far(4).start()
+    pass_on(a2, 1, short_parts(2))
+    share_far(1).start()
+    share_far(2).start()
+    pass_on(a2, 2, far_parts(2))
     pass_on(f1, 4)
     both(7, 8, near_part)
 
     logit_copy = remote(lg, lg_other, l_send, l_recv, sibling)
     logit_copy.start()
     both(3, 5, near_in)
+    pass_on(a2, 2, short_parts(2))
+    share_far(3).start()
+    share_far(4).start()
+    near_multiply(1, 2)
     far_multiply(1, 2)
-    pass_on(a2, 3)
+    pass_on(a2, 3, far_parts(2))
+    both(5, 7, near_in)
+    near_multiply(3, 2)
+    far_multiply(3, 2)
+    pass_on(a2, 3, short_parts(2))
     share_far(5).start()
     share_far(6).start()
-    near_multiply(1, 2)
-    both(5, 7, near_in)
-    far_multiply(3, 2)
-    near_multiply(3, 2)
+    near_in(7)
+    near_multiply(5, 2)
     pass_on(a2, 4)
     share_far(7).start()
-    near_in(7)
     far_multiply(5, 2)
-    near_multiply(5, 2)
+
+    def share_hidden(buffer, start, size, which):
+        rows = pl.ds(start, size)
+        return remote(
+            buffer.at[rows, pl.ds(0, HID)], buffer.at[rows, pl.ds(HID, HID)],
+            h_send.at[which], h_recv.at[which], sibling,
+        )
+
+    near_shares = [share_hidden(hn, start, size, which) for which, (start, size) in enumerate(N_PIECES)]
+    far_share = share_hidden(hf, 0, FR, 2)
+    share_near(7).wait_recv()
+    for share, (start, size) in zip(near_shares, N_PIECES):
+        stop = start + size
+        total = acc_n[start:stop, :] + jnp.dot(
+            jnp.concatenate([xn[7, 0, start:stop, :], xn[7, 1, start:stop, :]], axis=1),
+            w1[14 * W:16 * W, :], preferred_element_type=F32,
+        )
+        hn[start:stop, 0:HID] = jax.nn.gelu(total, approximate=True).astype(BF16)
+        share.start()
     far_multiply(7, 1)
-
-    def share_hidden(buffer, which):
-        return remote(
-            buffer.at[:, pl.ds(0, HID)], buffer.at[:, pl.ds(HID, HID)], h_send.at[which], h_recv.at[which], sibling,
-        )
-
     hf[:, 0:HID] = jax.nn.gelu(acc_f[...], approximate=True).astype(BF16)
-    share_hidden(hf, 1).start()
-    near_multiply(7, 1)
-    hn[:, 0:HID] = jax.nn.gelu(acc_n[...], approximate=True).astype(BF16)
-    share_hidden(hn, 0).start()
+    far_share.start()
     own_half, other_half = w2.at[:, pl.ds(0, HID)], w2.at[:, pl.ds(HID, HID)]
     pltpu.make_async_copy(own_half, own_half, w2_sem).wait()
     w2_all = remote(own_half, other_half, w2s_send, w2s_recv, sibling)
@@ -343,12 +369,13 @@
             send, recv.at[step - 1, way, half], along[way],
         )
 
-    bf = functools.partial(reduce_copy, pf, rf, F_HALF, bf_send, bf_recv)
-    bm = functools.partial(reduce_copy, pm, rm, M_HALF, bm_send, bm_recv)
+    bf = functools.partial(reduce_copy, pf, rf, F_PIECES, bf_send, bf_recv)
+    bm = functools.partial(reduce_copy, pm, rm, M_PIECES, bm_send, bm_recv)
 
     def reduce_step(transfer, own, received, halves, step, chosen=None):
-        for way, half in chosen or back_parts_of(step):
-            if step > 1 and (way, half) in back_parts_of(step - 1):
+        count = len(halves)
+        for way, half in chosen or back_parts_of(step, count):
+            if step > 1 and (way, half) in back_parts_of(step - 1, count):
                 transfer(step - 1, way, half).wait_recv()
                 start, size = halves[half]
                 slot = back_slot(step, way)
@@ -358,7 +385,11 @@
                 ).astype(BF16)
             transfer(step, way, half).start()
 
-    fresh, held = ((0, 1), (1, 0)), ((0, 0), (1, 1))
+    fresh, held = short_parts(2), far_parts(2)
+
+    def one_way(parts, which):
+        return [(way, half) for way, half in parts if way == which]
+
 
     def mix(slot):
         bn_all(slot).wait_recv()
@@ -367,14 +398,15 @@
     def mix_down(index):
         mix(7 - index)
 
-    share_hidden(hf, 1).wait_recv()
+    for share in near_shares:
+        share.wait_recv()
+    both(0, 1, near_out)
+    far_share.wait_recv()
     both(0, 1, far_out)
-    reduce_step(bf, pf, rf, F_HALF, 1)
+    reduce_step(bf, pf, rf, F_PIECES, 1)
     both(1, 3, far_out)
-    reduce_step(bf, pf, rf, F_HALF, 2, fresh)
-    share_hidden(hn, 0).wait_recv()
-    both(0, 2, near_out)
-    both(2, 3, near_out)
+    reduce_step(bf, pf, rf, F_PIECES, 2, fresh)
+    both(1, 3, near_out)
     logit_copy.wait()
     raised = jnp.exp(lg[...] + lg_other[...])
     probs = raised / jnp.sum(raised, axis=0, keepdims=True)
@@ -396,30 +428,31 @@
     cn[...] = weights(0, NR)
     cf[...] = weights(NR, FR)
 
+    both(3, 5, far_out)
+    reduce_step(bf, pf, rf, F_PIECES, 2, held)
     both(3, 4, near_out)
-    both(3, 5, far_out)
-    reduce_step(bf, pf, rf, F_HALF, 2, held)
+    reduce_step(bf, pf, rf, F_PIECES, 3, fresh)
+    both(0, 1, mix_down)
+    reduce_step(bm, pm, rm, M_PIECES, 1)
+    both(5, 7, far_out)
     both(4, 5, near_out)
-    reduce_step(bf, pf, rf, F_HALF, 3, fresh)
-    both(5, 7, far_out)
+    both(1, 2, mix_down)
+    reduce_step(bm, pm, rm, M_PIECES, 2, one_way(fresh, 0))
+    reduce_step(bf, pf, rf, F_PIECES, 3, held)
     both(5, 6, near_out)
-    both(0, 1, mix_down)
-    reduce_step(bm, pm, rm, M_HALF, 1)
+    reduce_step(bf, pf, rf, F_PIECES, 4, fresh)
+    both(2, 3, mix_down)
+    reduce_step(bm, pm, rm, M_PIECES, 2, one_way(fresh, 1))
+    reduce_step(bm, pm, rm, M_PIECES, 2, held)
     both(6, 7, near_out)
-    reduce_step(bf, pf, rf, F_HALF, 3, held)
-    reduce_step(bf, pf, rf, F_HALF, 4, fresh)
-    both(1, 2, mix_down)
-    reduce_step(bm, pm, rm, M_HALF, 2, fresh[:1])
+    both(7, 8, far_out)
+    both(3, 4, mix_down)
+    reduce_step(bf, pf, rf, F_PIECES, 4, held)
     both(7, 8, near_out)
-    both(2, 3, mix_down)
-    reduce_step(bm, pm, rm, M_HALF, 2, fresh[1:])
-    both(7, 8, far_out)
-    reduce_step(bm, pm, rm, M_HALF, 2, held)
-    reduce_step(bf, pf, rf, F_HALF, 4, held)
-    both(3, 5, mix_down)
-    reduce_step(bm, pm, rm, M_HALF, 3)
-
-    for way, half in back_parts_of(4):
+    both(4, 5, mix_down)
+    reduce_step(bm, pm, rm, M_PIECES, 3)
+
+    for way, half in back_parts_of(4, 2):
         bf(4, way, half).wait_recv()
     fr[...] = (
         pf[0].astype(F32) + rf[0, 3].astype(F32) + rf[1, 3].astype(F32)
@@ -432,11 +465,11 @@
     for p in FAR_ORDER:
         far_back(p).start()
     both(5, 7, mix_down)
-    reduce_step(bm, pm, rm, M_HALF, 4)
+    reduce_step(bm, pm, rm, M_PIECES, 4)
     both(7, 8, mix_down)
     remote(fr, ra, ra_send, ra_recv, sibling).wait_recv()
     far_term[...] = jnp.dot(cf[...], ra[...], preferred_element_type=F32) + pm[0].astype(F32)
-    for way, half in back_parts_of(4):
+    for way, half in back_parts_of(4, 2):
         bm(4, way, half).wait_recv()
     out[...] = (far_term[...] + rm[0, 3].astype(F32) + rm[1, 3].astype(F32)).astype(BF16)
 
@@ -455,8 +488,8 @@
     sent(pn.at[:, most], bn_send)
     sent(fr, ra_send)
     w2_all.wait_send()
-    share_hidden(hn, 0).wait_send()
-    share_hidden(hf, 1).wait_send()
+    for share in [*near_shares, far_share]:
+        share.wait_send()
 
 
 def layer(tokens, routing, gate_weight, expert_in, expert_out):
@@ -498,7 +531,7 @@
             pltpu.VMEM((2, GROUP), jnp.int32),
             dma, dma, dma, dma, dma, dma, dma,
             dma, dma((4, 2, 2)), dma, dma, dma, dma((Z,)), dma, dma((4, 2, 2)),
-            dma, dma((Z,)), dma, dma((Z,)), dma((2,)), dma((2,)), dma, dma,
+            dma, dma((Z,)), dma, dma((Z,)), dma((3,)), dma((3,)), dma, dma,
             dma, dma((4, 2, 2)), dma, dma((Z,)), dma, dma((4, 2, 2)), dma, dma,
         ],
         compiler_params=pltpu.CompilerParams(collective_id=0, has_side_effects=True),

time: 64 us -> 63.7 us (level)
  no operation moved by 1% of the time
where the time goes in v6:
time: 63.7 us; the launch traced here: 63.6 us
  Pallas kernels  62.9 us (99%)
  local copies, waits for them, and re-layouts  0.66 us (1%)
    pallas_call x1, Pallas kernels, layer(): pl.pallas_call(kernel, out_shape=pltpu.VMEM((GROUP, W), BF16), in_specs=[...  62.9 us

profile of v6, /device:TPU:1, one launch (start us, length us, event | category | flops | bytes accessed | tf_op | source)
XLA Modules:
  0.0 63.6 jit_solution(14382070758602159625)
XLA Ops:
  0.0 62.9 %experts.1 = bf16[256,256]{1,0:T(8,128)(2,1)S(1)} custom-call(bf16[256,256]{1,0:T(8,128)(2,1)} %tokens.1, s32[2,256]{1,0:T(2,128)} %bitcast.3, bf16[16,256]{1,0:T(8,128)(2,1)} %bitcast.2, bf16[1,4096,512]{2,1,0:T(8,128)(2,1)} %w_in.1, bf16[1,512,4096]{2,1,0:T(8,128)(2,1)} %w_out.1), custom_call_target="tpu_custom_call" | custom-call | tf_op jit(solution)/shard_map/experts/pallas_call | solution.py:499
  62.9 0.7 %copy.7 = bf16[256,256]{1,0:T(8,128)(2,1)} copy(bf16[256,256]{1,0:T(8,128)(2,1)S(1)} %experts.1) | data formatting | bytes 262144

commit v7 on v6

--- a/solution.py
+++ b/solution.py
@@ -17,12 +17,12 @@
 SHIFTS += [(2, 0), (0, 2), (2, -1), (2, 1), (2, 2), (-1, 2), (1, 2)]
 NEAR, FAR, SELF = 11, 5, 4
 NR, FR = NEAR * CAP, FAR * CAP
-NEAR_ORDER = [1, 3, 7, 5, 9, 10, 0, 8, 2, 6]
+NEAR_ORDER = [0, 8, 9, 10, 2, 6, 1, 3, 7, 5]
 FAR_ORDER = [13, 11, 14, 12, 15]
 TB = GROUP + EXPERTS
 T_PIECES = ((0, 128), (128, TB - 128))
 F_PIECES = ((0, 3 * CAP), (3 * CAP, FR - 3 * CAP))
-M_PIECES = ((0, 128), (128, 128))
+M_PIECES = ((0, 64), (64, 64), (128, 64), (192, 64))
 N_PIECES = ((0, 6 * CAP), (6 * CAP, NR - 6 * CAP))
 
 
@@ -60,7 +60,7 @@
 def kernel(
     tokens, picks, gate, w_in, w_out, out,
     tg, assign, near_send, far_send, xn, xf, acc_n, acc_f, w1, w2, hn, hf,
-    pf, rf, pn, rn, pm, rm, fr, ra, cn, cf, lg, lg_other, base, far_term, routing,
+    pf, rf, pn, rn, pm, rm, fr, ra, cn, cf, lg, lg_other, base, far_term, routing, first_near, first_far,
     tok_sem, gate_sem, picks_sem, w1_sem, w2_sem, w2s_send, w2s_recv,
     f1_send, f1_recv, a1_send, a1_recv, f2_send, f2_recv, a2_send, a2_recv,
     sn_send, sn_recv, sf_send, sf_recv, h_send, h_recv, l_send, l_recv,
@@ -225,8 +225,10 @@
     acc_n[...] = jnp.zeros_like(acc_n)
     acc_f[...] = jnp.zeros_like(acc_f)
 
+    none = lax.div(dp, X * Y)
+
     def both(lower, upper, work):
-        lax.fori_loop(lower, upper, lambda slot, carry: (work(slot), carry)[1], 0)
+        lax.fori_loop(lower + none, upper + none, lambda slot, carry: (work(slot), carry)[1], 0)
 
     def near_part(slot):
         dispatch_near(slot)
@@ -352,7 +354,9 @@
 
     def near_out(index):
         slot = 7 - index
-        terms = second(hn, slot)
+        send_back(slot, second(hn, slot))
+
+    def send_back(slot, terms):
         pn[slot] = terms
         rn[slot, SELF * CAP:(SELF + 1) * CAP, :] = terms[SELF * CAP:(SELF + 1) * CAP, :]
         for p in NEAR_ORDER:
@@ -398,11 +402,19 @@
     def mix_down(index):
         mix(7 - index)
 
+    def own_part(buffer):
+        return jnp.dot(buffer[:, 0:HID], w2[7, 0:HID, :], preferred_element_type=F32)
+
+    def other_part(buffer):
+        return jnp.dot(buffer[:, HID:2 * HID], w2[7, HID:2 * HID, :], preferred_element_type=F32)
+
+    first_near[...] = own_part(hn)
+    first_far[...] = own_part(hf)
     for share in near_shares:
         share.wait_recv()
-    both(0, 1, near_out)
+    send_back(7, (first_near[...] + other_part(hn)).astype(BF16))
     far_share.wait_recv()
-    both(0, 1, far_out)
+    pf[7] = (first_far[...] + other_part(hf)).astype(BF16)
     reduce_step(bf, pf, rf, F_PIECES, 1)
     both(1, 3, far_out)
     reduce_step(bf, pf, rf, F_PIECES, 2, fresh)
@@ -437,13 +449,13 @@
     both(5, 7, far_out)
     both(4, 5, near_out)
     both(1, 2, mix_down)
-    reduce_step(bm, pm, rm, M_PIECES, 2, one_way(fresh, 0))
+    reduce_step(bm, pm, rm, M_PIECES, 2, one_way(short_parts(4), 0))
     reduce_step(bf, pf, rf, F_PIECES, 3, held)
     both(5, 6, near_out)
     reduce_step(bf, pf, rf, F_PIECES, 4, fresh)
     both(2, 3, mix_down)
-    reduce_step(bm, pm, rm, M_PIECES, 2, one_way(fresh, 1))
-    reduce_step(bm, pm, rm, M_PIECES, 2, held)
+    reduce_step(bm, pm, rm, M_PIECES, 2, one_way(short_parts(4), 1))
+    reduce_step(bm, pm, rm, M_PIECES, 2, far_parts(4))
     both(6, 7, near_out)
     both(7, 8, far_out)
     both(3, 4, mix_down)
@@ -452,6 +464,7 @@
     both(4, 5, mix_down)
     reduce_step(bm, pm, rm, M_PIECES, 3)
 
+    both(5, 6, mix_down)
     for way, half in back_parts_of(4, 2):
         bf(4, way, half).wait_recv()
     fr[...] = (
@@ -464,12 +477,12 @@
 
     for p in FAR_ORDER:
         far_back(p).start()
-    both(5, 7, mix_down)
+    both(6, 7, mix_down)
     reduce_step(bm, pm, rm, M_PIECES, 4)
     both(7, 8, mix_down)
     remote(fr, ra, ra_send, ra_recv, sibling).wait_recv()
     far_term[...] = jnp.dot(cf[...], ra[...], preferred_element_type=F32) + pm[0].astype(F32)
-    for way, half in back_parts_of(4, 2):
+    for way, half in back_parts_of(4, 4):
         bm(4, way, half).wait_recv()
     out[...] = (far_term[...] + rm[0, 3].astype(F32) + rm[1, 3].astype(F32)).astype(BF16)
 
@@ -529,10 +542,12 @@
             pltpu.VMEM((8, GROUP), F32),
             pltpu.VMEM((GROUP, W), F32),
             pltpu.VMEM((2, GROUP), jnp.int32),
+            pltpu.VMEM((NR, W), F32),
+            pltpu.VMEM((FR, W), F32),
             dma, dma, dma, dma, dma, dma, dma,
             dma, dma((4, 2, 2)), dma, dma, dma, dma((Z,)), dma, dma((4, 2, 2)),
             dma, dma((Z,)), dma, dma((Z,)), dma((3,)), dma((3,)), dma, dma,
-            dma, dma((4, 2, 2)), dma, dma((Z,)), dma, dma((4, 2, 2)), dma, dma,
+            dma, dma((4, 2, 2)), dma, dma((Z,)), dma, dma((4, 2, 4)), dma, dma,
         ],
         compiler_params=pltpu.CompilerParams(collective_id=0, has_side_effects=True),
         name="experts",

time: 63.7 us -> 63.2 us (level)
  no operation moved by 1% of the time
where the time goes in v7:
time: 63.2 us; the launch traced here: 63.1 us
  Pallas kernels  62.4 us (99%)
  local copies, waits for them, and re-layouts  0.66 us (1%)
    pallas_call x1, Pallas kernels, layer(): pl.pallas_call(kernel, out_shape=pltpu.VMEM((GROUP, W), BF16), in_specs=[...  62.4 us

profile of v7, /device:TPU:1, one launch (start us, length us, event | category | flops | bytes accessed | tf_op | source)
XLA Modules:
  0.0 63.1 jit_solution(9029923492188307366)
XLA Ops:
  0.0 62.4 %experts.1 = bf16[256,256]{1,0:T(8,128)(2,1)S(1)} custom-call(bf16[256,256]{1,0:T(8,128)(2,1)} %tokens.1, s32[2,256]{1,0:T(2,128)} %bitcast.3, bf16[16,256]{1,0:T(8,128)(2,1)} %bitcast.2, bf16[1,4096,512]{2,1,0:T(8,128)(2,1)} %w_in.1, bf16[1,512,4096]{2,1,0:T(8,128)(2,1)} %w_out.1), custom_call_target="tpu_custom_call" | custom-call | tf_op jit(solution)/shard_map/experts/pallas_call | solution.py:512
  62.4 0.7 %copy.7 = bf16[256,256]{1,0:T(8,128)(2,1)} copy(bf16[256,256]{1,0:T(8,128)(2,1)S(1)} %experts.1) | data formatting | bytes 262144

commit v8 on v7

--- a/solution.py
+++ b/solution.py
@@ -452,10 +452,10 @@
     reduce_step(bm, pm, rm, M_PIECES, 2, one_way(short_parts(4), 0))
     reduce_step(bf, pf, rf, F_PIECES, 3, held)
     both(5, 6, near_out)
-    reduce_step(bf, pf, rf, F_PIECES, 4, fresh)
     both(2, 3, mix_down)
     reduce_step(bm, pm, rm, M_PIECES, 2, one_way(short_parts(4), 1))
     reduce_step(bm, pm, rm, M_PIECES, 2, far_parts(4))
+    reduce_step(bf, pf, rf, F_PIECES, 4, fresh)
     both(6, 7, near_out)
     both(7, 8, far_out)
     both(3, 4, mix_down)

time: 63.2 us -> 63.2 us (level)
  no operation moved by 1% of the time
where the time goes in v8:
time: 63.2 us; the launch traced here: 63.1 us
  Pallas kernels  62.4 us (99%)
  local copies, waits for them, and re-layouts  0.66 us (1%)
    pallas_call x1, Pallas kernels, layer(): pl.pallas_call(kernel, out_shape=pltpu.VMEM((GROUP, W), BF16), in_specs=[...  62.4 us

profile of v8, /device:TPU:1, one launch (start us, length us, event | category | flops | bytes accessed | tf_op | source)
XLA Modules:
  0.0 63.1 jit_solution(17601021577451151234)
XLA Ops:
  0.0 62.4 %experts.1 = bf16[256,256]{1,0:T(8,128)(2,1)S(1)} custom-call(bf16[256,256]{1,0:T(8,128)(2,1)} %tokens.1, s32[2,256]{1,0:T(2,128)} %bitcast.3, bf16[16,256]{1,0:T(8,128)(2,1)} %bitcast.2, bf16[1,4096,512]{2,1,0:T(8,128)(2,1)} %w_in.1, bf16[1,512,4096]{2,1,0:T(8,128)(2,1)} %w_out.1), custom_call_target="tpu_custom_call" | custom-call | tf_op jit(solution)/shard_map/experts/pallas_call | solution.py:512
  62.4 0.7 %copy.7 = bf16[256,256]{1,0:T(8,128)(2,1)} copy(bf16[256,256]{1,0:T(8,128)(2,1)S(1)} %experts.1) | data formatting | bytes 262144
